TPU v7x, 256 devices: a whole 4x4x8 slice. The times are simulated.
256 devices in a mesh: freq: 4 (over x_hi, core), rcv: 64 (over y, z, x_lo).
Axes of the slice: x: 4 (x_hi: 2, x_lo: 2; x = x_hi * 2 + x_lo), y: 4, z: 8, core: 2. Of those that a mesh axis runs over, the one named last changes fastest.
Arguments:
- reflection: bfloat16 [8, 2, 2560, 2560], P('freq', None, 'rcv'), may hold values from -5 to 5, as said below
- starts: int32 [2560, 192], P('rcv'), may hold values from 8 to 56
- focusing: float32 [8, 2560, 2, 192], P('freq', 'rcv'), may hold values from -6 to 6
- residual: float32 [8, 2560, 2, 192], P('freq', 'rcv'), may hold values from -6 to 6
- direction: float32 [8, 2560, 2, 192], P('freq', 'rcv'), may hold values from -6 to 6
- gradient: float32 [8, 2560, 2, 192], P('freq', 'rcv'), may hold values from -30 to 30
Outputs:
- new_focusing: float32 [8, 2560, 2, 192], P('freq', 'rcv')
- new_residual: float32 [8, 2560, 2, 192], P('freq', 'rcv')
- new_direction: float32 [8, 2560, 2, 192], P('freq', 'rcv')
- green_field: float32 [8, 2560, 2, 192], P('freq', 'rcv')
- focal_correlation: float32 [8, 2, 192], P('freq')
Inputs may be any that keep to these rules, and one draw needn't show every extreme that they name: Each frequency's matrix is symmetric in source and receiver: reflection[f, c, s, r] = reflection[f, c, r, s].
All inputs are finite; a program needn't handle non-finite values.
Results may differ from a plain program's by a relative error of at most 0.0003.
The roundings to bfloat16 on the way count: a program that leaves them out, or rounds other values in their place, can miss the bound.
Values may be sent and summed in bfloat16 or wider, within the bound.
A program may use at most 64 MiB of HBM per device.

v0:
```python
import math

import jax
import jax.numpy as jnp
from jax import lax
from jax.sharding import Mesh
from jax.sharding import PartitionSpec as P

N = 2560
F = 8
TS = 64
FREQ = ("freq_0", "freq_1")
RCV = ("rcv_0", "rcv_1", "rcv_2")
FREQ_RCV = ("freq_0", "freq_1", "rcv_0", "rcv_1", "rcv_2")


band_start = 5
tiny = 1e-06
highest = lax.Precision.HIGHEST


def in_order(pieces, dim):
    lengths = list(pieces.shape[1:])
    lengths[dim] *= pieces.shape[0]
    return jnp.moveaxis(pieces, 0, dim).reshape(lengths)


def sent_to_all(value, axis):
    count = lax.axis_size(axis)
    return lax.all_to_all(
        jnp.broadcast_to(value[None], (count, *value.shape)), axis, 0, 0, tiled=True
    )


def gather_directly(value, axis, dim):
    return in_order(sent_to_all(value, axis), dim)


def one_axis_at_a_time(value, axes):
    for axis in axes:
        value = lax.psum(value, axis)
    return value


def all_blocks(value, axes, sequence):
    pieces = value
    for k in sequence:
        pieces = lax.all_gather(pieces, axes[k])
    done = sequence[::-1]
    back = [done.index(k) for k in range(len(axes))]
    pieces = pieces.transpose(*back, *range(len(axes), pieces.ndim))
    return pieces.reshape(-1, *value.shape)


def gathered_by_axis(value, axes, sequence, dim):
    return in_order(all_blocks(value, axes, sequence), dim)


def of_everyone(value, axis):
    everything = sent_to_all(value, axis)
    return jnp.sum(everything, axis=0)


def tables(count, offset):
    times = jnp.arange(TS, dtype=jnp.float32)[:, None]
    bins = (jnp.arange(count, dtype=jnp.int32) + offset + band_start).astype(jnp.float32)[None, :]
    phase = 2.0 * jnp.pi * times * bins / TS
    return (jnp.cos(phase), jnp.sin(phase))


def contract_time(table, values):
    return jnp.einsum("tf,frk->trk", table, values, precision=highest)


def contract_back(table, values):
    return jnp.einsum("tf,trk->frk", table, values, precision=highest)


def time_gate(field, forward_cos, forward_sin, back_cos, back_sin, limits, complement):
    real_part = field[:, :, 0]
    imag_part = field[:, :, 1]
    time_real = contract_time(forward_cos, real_part) - contract_time(forward_sin, imag_part)
    time_imag = contract_time(forward_sin, real_part) + contract_time(forward_cos, imag_part)
    clock = jnp.arange(TS, dtype=jnp.int32)[:, None, None]
    window = (clock < limits[None]).astype(jnp.float32)
    if complement:
        window = 1.0 - window
    kept_real = window * time_real
    kept_imag = window * time_imag
    out_real = (contract_back(back_cos, kept_real) + contract_back(back_sin, kept_imag)) / TS
    out_imag = (contract_back(back_cos, kept_imag) - contract_back(back_sin, kept_real)) / TS
    return jnp.stack([out_real, out_imag], axis=2)


def combine(total, conjugate):
    if conjugate:
        out_real = total[:, 0, :, 0] + total[:, 1, :, 1]
        out_imag = total[:, 0, :, 1] - total[:, 1, :, 0]
    else:
        out_real = total[:, 0, :, 0] - total[:, 1, :, 1]
        out_imag = total[:, 0, :, 1] + total[:, 1, :, 0]
    return jnp.stack([out_real, out_imag], axis=2)


def per_device(reflection, starts, focusing, residual, direction, gradient):
    local_freq = reflection.shape[0]
    position = lax.axis_index(FREQ)
    cos_table, sin_table = tables(F, 0)
    own_cos, own_sin = tables(local_freq, position * local_freq)

    def gate(field, complement):
        whole = gather_directly(field, FREQ, 0)
        return time_gate(whole, cos_table, sin_table, own_cos, own_sin, starts, complement)

    def accumulate(piece):
        return jnp.einsum("fpnm,fmqk->fpnqk", reflection, piece, preferred_element_type=jnp.float32)

    direction_low = direction.astype(jnp.bfloat16)
    focusing_low = focusing.astype(jnp.bfloat16)
    aimed_total = accumulate(lax.all_gather(direction_low, RCV, axis=1, tiled=True))
    direction_image = combine(aimed_total, False)
    image = gate(direction_image, False)
    gamma, curvature = (
        one_axis_at_a_time(jnp.sum(gradient * gradient), FREQ_RCV),
        one_axis_at_a_time(jnp.sum(image * image), FREQ_RCV),
    )
    alpha = gamma / (curvature + tiny)
    new_focusing = focusing + alpha * direction
    new_residual = residual - alpha * image
    gated = gate(new_residual, False).astype(jnp.bfloat16)
    total = accumulate(gathered_by_axis(gated, RCV, (2, 0, 1), 1))
    new_gradient = combine(total, True)
    new_gamma = one_axis_at_a_time(jnp.sum(new_gradient * new_gradient), FREQ_RCV)
    new_direction = new_gradient + new_gamma / (gamma + tiny) * direction
    focus_total = accumulate(lax.all_gather(focusing_low, RCV, axis=1, tiled=True))
    focusing_image = combine(focus_total, False)
    green_field = gate(focusing_image + alpha * direction_image, True)
    corr_real = jnp.sum(
        green_field[:, :, 0] * new_focusing[:, :, 0] + green_field[:, :, 1] * new_focusing[:, :, 1],
        axis=1,
    )
    corr_imag = jnp.sum(
        green_field[:, :, 1] * new_focusing[:, :, 0] - green_field[:, :, 0] * new_focusing[:, :, 1],
        axis=1,
    )
    partial_corr = jnp.stack([corr_real, corr_imag], axis=1)
    focal_correlation = of_everyone(partial_corr, RCV) / math.sqrt(N)
    return (new_focusing, new_residual, new_direction, green_field, focal_correlation)


def solution(mesh):
    finer = Mesh(
        mesh.devices.reshape(2, 2, 4, 8, 2), ("freq_0", "freq_1", "rcv_0", "rcv_1", "rcv_2")
    )
    in_specs = (
        P(FREQ, None, RCV, None),
        P(RCV, None),
        P(FREQ, RCV, None, None),
        P(FREQ, RCV, None, None),
        P(FREQ, RCV, None, None),
        P(FREQ, RCV, None, None),
    )
    out_specs = (
        P(FREQ, RCV, None, None),
        P(FREQ, RCV, None, None),
        P(FREQ, RCV, None, None),
        P(FREQ, RCV, None, None),
        P(FREQ, None, None),
    )
    return jax.shard_map(
        per_device, mesh=finer, in_specs=in_specs, out_specs=out_specs, check_vma=False
    )
```

profile of v0, /device:TPU:32, one launch (start us, length us, event | category | flops | bytes accessed | tf_op | source)
XLA Modules:
  0.0 781.0 jit_solution(11673476122548457123)
XLA Ops:
  7.2 1.6 copy.290
  8.9 1.6 copy.289
  10.5 307.1 %all-gather.6.cloned.1.call-done = bf16[2,2560,2,192]{3,1,2,0:T(8,128)(2,1)} async-done(((bf16[2,40,2,192]{3,1,2,0:T(8,128)(2,1)}), bf16[2,2560,2,192]{3,1,2,0:T(8,128)(2,1)}) %all-gather.6.cloned.1.call-update) | async-done | bytes 3932176 | tf_op jit(solution)/shard_map/all_gather | solution.py:120
  317.6 3.5 fusion
  322.3 4.4 all-to-all-start
  327.5 16.5 %all-to-all-done = f32[4,2,40,2,192]{4,1,2,3,0:T(2,128)S(1)} async-done(((f32[4,2,40,2,192]{4,1,2,3,0:T(2,128)}), f32[4,2,40,2,192]{4,1,2,3,0:T(2,128)S(1)}, u32[]{:S(2)}, u32[]{:S(2)}) %all-to-all-start) | async-done | bytes 491552 | tf_op jit(solution)/shard_map/all_to_all | solution.py:30
  344.6 2.4 fusion.7
  347.0 2.5 add_select_fusion.1
  349.6 1.4 fusion.115
  352.3 2.4 fusion.8
  354.7 2.5 subtract_select_fusion.1
  357.3 1.8 fusion.103
  361.2 7.3 all-reduce.4
  368.5 3.1 all-reduce.3
  371.6 8.3 %all-reduce.1 = (f32[]{:T(128)}, f32[]{:T(128)}) all-reduce(f32[]{:T(128)} %get-tuple-element.38, f32[]{:T(128)} %get-tuple-element.39), channel_id=1, replica_groups=mesh['freq_0'=2,'freq_1'=2,'rcv_0'=4,'rcv_1'=8,'rcv_2'=2] {'rcv_0'}, use_global_device_ids=true, to_apply=%region_3.0 | all-reduce | flops 2 | bytes 16 | tf_op jit(solution)/shard_map/psum | solution.py:41
  379.9 17.1 %all-reduce = (f32[]{:T(128)}, f32[]{:T(128)}) all-reduce(f32[]{:T(128)} %get-tuple-element.34, f32[]{:T(128)} %get-tuple-element.35), channel_id=1, replica_groups=mesh['freq_0'=2,'freq_1'=2,'rcv_0'=4,'rcv_1'=8,'rcv_2'=2] {'rcv_1'}, use_global_device_ids=true, to_apply=%region_4.0 | all-reduce | flops 2 | bytes 16 | tf_op jit(solution)/shard_map/psum | solution.py:41
  397.0 5.5 all-reduce.2
  404.8 19.1 %all_to_all.20 = f32[4,2,40,2,192]{4,1,2,3,0:T(2,128)S(1)} all-to-all(f32[4,2,40,2,192]{4,1,2,3,0:T(2,128)S(1)} %broadcast_in_dim.9), channel_id=1, replica_groups=mesh['freq_0'=2,'freq_1'=2,'rcv_0'=4,'rcv_1'=8,'rcv_2'=2] {'freq_0','fre..., dimensions={0} | all-to-all | bytes 983040 | tf_op jit(solution)/shard_map/all_to_all | solution.py:30
  424.7 2.4 fusion.10
  427.0 2.5 subtract_select_fusion
  429.6 1.4 fusion.99
  431.0 2.4 fusion.9
  433.3 2.5 add_select_fusion
  437.3 1.6 fusion.101
  440.3 6.2 all_gather.23
  446.5 14.5 %all-gather = bf16[8,2,40,2,192]{4,2,3,1,0:T(8,128)(2,1)} all-gather(bf16[2,2,40,2,192]{4,2,3,1,0:T(8,128)(2,1)S(1)} %all_gather.23), channel_id=2, replica_groups=mesh['freq_0'=2,'freq_1'=2,'rcv_0'=4,'rcv_1'=8,'rcv_2'=2] {'rcv_0'}, dimensions={0}, use_global_device_ids=true | all-gather | bytes 614400 | tf_op jit(solution)/shard_map/all_gather | solution.py:48
  461.0 161.6 %all-gather.8.cloned.1.call-done = bf16[2,2560,2,192]{3,1,2,0:T(8,128)(2,1)} async-done(((bf16[2,40,2,192]{3,1,2,0:T(8,128)(2,1)}), bf16[2,2560,2,192]{3,1,2,0:T(8,128)(2,1)}) %all-gather.8.cloned.1.call-update) | async-done | bytes 3932176 | tf_op jit(solution)/shard_map/all_gather | solution.py:135
  622.6 3.5 fusion.2
  627.3 3.6 all-to-all-start.2
  631.6 11.1 %all-to-all-done.2 = f32[4,2,40,2,192]{4,1,2,3,0:T(2,128)S(1)} async-done(((f32[4,2,40,2,192]{4,1,2,3,0:T(2,128)}), f32[4,2,40,2,192]{4,1,2,3,0:T(2,128)S(1)}, u32[]{:S(2)}, u32[]{:S(2)}) %all-to-all-start.2) | async-done | bytes 491552 | tf_op jit(solution)/shard_map/all_to_all | solution.py:30
  643.4 2.4 fusion.11
  645.8 3.9 fusion.12
  649.6 3.7 add_multiply_fusion
  653.3 31.4 %all-gather.10.cloned.1.call-done = bf16[32,2,2,40,2,192]{5,3,4,2,1,0:T(8,128)(2,1)} async-done(((bf16[4,2,2,40,2,192]{5,3,4,2,1,0:T(8,128)(2,1)}), bf16[32,2,2,40,2,192]{5,3,4,2,1,0:T(8,128)(2,1)}) %all-gather.10.cloned.1.call-update) | async-done | bytes 3932176 | tf_op jit(solution)/shard_map/all_gather | solution.py:48
  684.7 3.0 copy.180
  690.7 4.3 subtract_multiply_fusion
  695.0 7.0 psum.115
  702.0 3.8 fusion.109
  705.8 3.3 psum.116
  709.1 3.7 fusion.95
  712.8 11.1 %psum.117 = f32[]{:T(128)} all-reduce(f32[]{:T(128)} %psum.116), channel_id=1, replica_groups=mesh['freq_0'=2,'freq_1'=2,'rcv_0'=4,'rcv_1'=8,'rcv_2'=2] {'rcv_0'}, use_global_device_ids=true, to_apply=%region_15.0 | all-reduce | flops 1 | bytes 8 | tf_op jit(solution)/shard_map/psum | solution.py:41
  723.9 2.0 fusion.97
  725.9 17.0 %psum.118 = f32[]{:T(128)} all-reduce(f32[]{:T(128)} %psum.117), channel_id=1, replica_groups=mesh['freq_0'=2,'freq_1'=2,'rcv_0'=4,'rcv_1'=8,'rcv_2'=2] {'rcv_1'}, use_global_device_ids=true, to_apply=%region_16.0 | all-reduce | flops 1 | bytes 8 | tf_op jit(solution)/shard_map/psum | solution.py:41
  743.0 2.0 fusion.107
  745.0 5.5 psum.119
  754.2 8.7 %all-to-all-start.3 = ((f32[64,2,2,192]{3,2,1,0:T(2,128)}), f32[64,2,2,192]{3,2,1,0:T(2,128)S(1)}, u32[]{:S(2)}, u32[]{:S(2)}) async-start(f32[64,2,2,192]{3,2,1,0:T(2,128)} %broadcast_in_dim.11), calls=%async_computation.3 | async-start | bytes 524288 | tf_op jit(solution)/shard_map/all_to_all | solution.py:30
  762.9 1.7 copy.198
  767.0 6.5 all-to-all-done.3
  (74 shorter events, 21.5 us)
Async XLA Ops:
  7.2 310.4 %copy-start = (bf16[2,2,40,2560]{3,2,1,0:T(8,128)(2,1)S(1)}, bf16[2,2,40,2560]{3,2,1,0:T(8,128)(2,1)}, u32[]{:S(2)}) copy-start(bf16[2,2,40,2560]{3,2,1,0:T(8,128)(2,1)} %param.6) | copy-start | bytes 2457604
  7.2 310.4 %all-gather.6.cloned.1.call-start = ((), (), s32[]{:S(2)}) async-start(), calls=%async_computation.4 | async-start | bytes 5324800 | tf_op jit(solution)/shard_map/all_gather | solution.py:120
  8.9 613.7 %all-gather.8.cloned.1.call-start = ((), (), s32[]{:S(2)}) async-start(), calls=%async_computation.5 | async-start | bytes 5324800 | tf_op jit(solution)/shard_map/all_gather | solution.py:135
  321.1 5.6 copy-start.8
  322.3 21.7 %all-to-all-start = ((f32[4,2,40,2,192]{4,1,2,3,0:T(2,128)}), f32[4,2,40,2,192]{4,1,2,3,0:T(2,128)S(1)}, u32[]{:S(2)}, u32[]{:S(2)}) async-start(f32[4,2,40,2,192]{4,1,2,3,0:T(2,128)} %broadcast_in_dim.8), calls=%async_computation | async-start | bytes 1310720 | tf_op jit(solution)/shard_map/all_to_all | solution.py:30
  326.6 358.1 %all-gather.10.cloned.1.call-start = ((), (), s32[]{:S(2)}) async-start(), calls=%async_computation.6 | async-start | bytes 5898240 | tf_op jit(solution)/shard_map/all_gather | solution.py:48
  327.5 19.5 %copy-start.4 = (s32[40,192]{1,0:T(8,128)S(1)}, s32[40,192]{1,0:T(8,128)}, u32[]{:S(2)}) copy-start(s32[40,192]{1,0:T(8,128)} %param.7) | copy-start | bytes 92164
  357.2 46.6 %copy-start.9 = (f32[2,40,2,192]{3,2,1,0:T(2,128)S(1)}, f32[2,40,2,192]{3,2,1,0:T(2,128)}, u32[]{:S(2)}) copy-start(f32[2,40,2,192]{3,2,1,0:T(2,128)} %param.9) | copy-start | bytes 368644
  403.9 0.7 copy-start.5
  627.3 15.4 %all-to-all-start.2 = ((f32[4,2,40,2,192]{4,1,2,3,0:T(2,128)}), f32[4,2,40,2,192]{4,1,2,3,0:T(2,128)S(1)}, u32[]{:S(2)}, u32[]{:S(2)}) async-start(f32[4,2,40,2,192]{4,1,2,3,0:T(2,128)} %broadcast_in_dim.10), calls=%async_computation.2 | async-start | bytes 1310720 | tf_op jit(solution)/shard_map/all_to_all | solution.py:30
  643.4 2.4 copy-start.2
  687.7 3.0 copy-start.1
  687.7 3.0 copy-start.3
  688.8 0.6 copy-start.6
  689.4 0.6 copy-start.7
  754.2 19.3 %all-to-all-start.3 = ((f32[64,2,2,192]{3,2,1,0:T(2,128)}), f32[64,2,2,192]{3,2,1,0:T(2,128)S(1)}, u32[]{:S(2)}, u32[]{:S(2)}) async-start(f32[64,2,2,192]{3,2,1,0:T(2,128)} %broadcast_in_dim.11), calls=%async_computation.3 | async-start | bytes 524288 | tf_op jit(solution)/shard_map/all_to_all | solution.py:30
Sparse Core Ops, SparseCore 0:
  10.4 307.1 all-gather.5
  319.9 302.6 all-gather.7
  624.4 60.2 all-gather.9
where the time goes:
time: 792 us; the launch traced here: 781 us
  waiting for transfers between devices  534 us (67%)
  blocking collectives  125 us (16%)
  matrix products  65.1 us (8%)
  local copies, waits for them, and re-layouts  17.5 us (2%)
  between operations  17 us (2%)
  starting transfers between devices  16.8 us (2%)
    all_gather x1, waiting for transfers between devices, per_device(): lax.all_gather(direction_low, RCV, axis=1, tiled=True)  307 us
    all_gather x1, waiting for transfers between devices, per_device(): lax.all_gather(focusing_low, RCV, axis=1, tiled=True)  162 us
    psum x10, blocking collectives, one_axis_at_a_time(): value = lax.psum(value, axis)  85.4 us
    all_to_all x3, waiting for transfers between devices, sent_to_all(): lax.all_to_all(jnp.broadcast_to(value[None], (count, *value.shape)), axis...  34.1 us
    dot_general x12, matrix products, contract_time(): return jnp.einsum('tf,frk->trk', table, values, precision=highest)  33.8 us
    all_gather x1, waiting for transfers between devices, all_blocks(): pieces = lax.all_gather(pieces, axes[k])  31.4 us
    dot_general x12, matrix products, contract_back(): return jnp.einsum('tf,trk->frk', table, values, precision=highest)  23.3 us
    all_gather x2, blocking collectives, all_blocks(): pieces = lax.all_gather(pieces, axes[k])  20.7 us
  transfers between devices with their start and end apart: 6, of which 6 were waited for; matrix products, arithmetic and copies ran while one was open for 8% of the time, Pallas kernels for 0%

commit v1 on v0

--- a/solution.py
+++ b/solution.py
@@ -117,7 +117,7 @@
 
     direction_low = direction.astype(jnp.bfloat16)
     focusing_low = focusing.astype(jnp.bfloat16)
-    aimed_total = accumulate(lax.all_gather(direction_low, RCV, axis=1, tiled=True))
+    aimed_total = accumulate(gathered_by_axis(direction_low, RCV, (2, 0, 1), 1))
     direction_image = combine(aimed_total, False)
     image = gate(direction_image, False)
     gamma, curvature = (
@@ -132,7 +132,7 @@
     new_gradient = combine(total, True)
     new_gamma = one_axis_at_a_time(jnp.sum(new_gradient * new_gradient), FREQ_RCV)
     new_direction = new_gradient + new_gamma / (gamma + tiny) * direction
-    focus_total = accumulate(lax.all_gather(focusing_low, RCV, axis=1, tiled=True))
+    focus_total = accumulate(gathered_by_axis(focusing_low, RCV, (2, 0, 1), 1))
     focusing_image = combine(focus_total, False)
     green_field = gate(focusing_image + alpha * direction_image, True)
     corr_real = jnp.sum(

time: 792 us -> 386 us (0.49)
  waiting for transfers between devices: 534 us -> 101 us
  blocking collectives: 125 us -> 160 us
    all_gather x2 -> x0, waiting for transfers between devices: 469 us -> none  [the longest x1 307 us: per_device(): lax.all_gather(direction_low, RCV, axis=1, tiled=True)]
    all_gather x1 -> x3, waiting for transfers between devices: 31.4 us -> 73 us  [all_blocks(): pieces = lax.all_gather(pieces, axes[k])]
    all_gather x2 -> x6, blocking collectives: 20.7 us -> 58.2 us  [all_blocks(): pieces = lax.all_gather(pieces, axes[k])]
  transfers between devices with their start and end apart: 6 -> 6, of which waited for: 6 -> 5; matrix products, arithmetic and copies ran while one was open for 8% -> 16% of each run, Pallas kernels for 0% -> 0%
where the time goes in v1:
time: 386 us; the launch traced here: 382 us
  blocking collectives  160 us (41%)
  waiting for transfers between devices  101 us (26%)
  matrix products  58.4 us (15%)
  local copies, waits for them, and re-layouts  21.5 us (6%)
  between operations  17.1 us (4%)
  starting transfers between devices  16.6 us (4%)
  other arithmetic  6.69 us (2%)
    psum x10, blocking collectives, one_axis_at_a_time(): value = lax.psum(value, axis)  87.9 us
    all_gather x3, waiting for transfers between devices, all_blocks(): pieces = lax.all_gather(pieces, axes[k])  73 us
    all_gather x6, blocking collectives, all_blocks(): pieces = lax.all_gather(pieces, axes[k])  58.2 us
    dot_general x12, matrix products, contract_time(): return jnp.einsum('tf,frk->trk', table, values, precision=highest)  33.8 us
    all_to_all x3, waiting for transfers between devices, sent_to_all(): lax.all_to_all(jnp.broadcast_to(value[None], (count, *value.shape)), axis...  28.3 us
    dot_general x12, matrix products, contract_back(): return jnp.einsum('tf,trk->frk', table, values, precision=highest)  21.5 us
    all_to_all x3, starting transfers between devices, sent_to_all(): lax.all_to_all(jnp.broadcast_to(value[None], (count, *value.shape)), axis...  16.4 us
    all_to_all x1, blocking collectives, sent_to_all(): lax.all_to_all(jnp.broadcast_to(value[None], (count, *value.shape)), axis...  14.1 us
  transfers between devices with their start and end apart: 6, of which 5 were waited for; matrix products, arithmetic and copies ran while one was open for 16% of the time, Pallas kernels for 0%

profile of v1, /device:TPU:32, one launch (start us, length us, event | category | flops | bytes accessed | tf_op | source)
XLA Modules:
  0.0 381.9 jit_solution(1641912904431672006)
XLA Ops:
  8.2 5.1 %all-gather = bf16[4,40,2,192]{3,1,2,0:T(8,128)(2,1)S(1)} all-gather(bf16[2,40,2,192]{3,1,2,0:T(8,128)(2,1)S(1)} %copy.354), channel_id=2, replica_groups=mesh['freq_0'=2,'freq_1'=2,'rcv_0'=4,'rcv_1'=8,'rcv_2'=2] {'rcv_2'}, dimensions={0}, use_global_device_ids=true | all-gather | bytes 184320 | tf_op jit(solution)/shard_map/all_gather | solution.py:48
  13.3 14.6 %all-gather.1 = bf16[8,2,40,2,192]{4,2,3,1,0:T(8,128)(2,1)} all-gather(bf16[2,2,40,2,192]{4,2,3,1,0:T(8,128)(2,1)S(1)} %bitcast.214), channel_id=3, replica_groups=mesh['freq_0'=2,'freq_1'=2,'rcv_0'=4,'rcv_1'=8,'rcv_2'=2] {'rcv_0'}, dimensions={0}, use_global_device_ids=true | all-gather | bytes 614400 | tf_op jit(solution)/shard_map/all_gather | solution.py:48
  29.0 5.1 %all-gather.5 = bf16[4,40,2,192]{3,1,2,0:T(8,128)(2,1)S(1)} all-gather(bf16[2,40,2,192]{3,1,2,0:T(8,128)(2,1)S(1)} %copy.353), channel_id=7, replica_groups=mesh['freq_0'=2,'freq_1'=2,'rcv_0'=4,'rcv_1'=8,'rcv_2'=2] {'rcv_2'}, dimensions={0}, use_global_device_ids=true | all-gather | bytes 184320 | tf_op jit(solution)/shard_map/all_gather | solution.py:48
  34.1 14.4 %all-gather.6 = bf16[8,2,40,2,192]{4,2,3,1,0:T(8,128)(2,1)} all-gather(bf16[2,2,40,2,192]{4,2,3,1,0:T(8,128)(2,1)S(1)} %bitcast.215), channel_id=8, replica_groups=mesh['freq_0'=2,'freq_1'=2,'rcv_0'=4,'rcv_1'=8,'rcv_2'=2] {'rcv_0'}, dimensions={0}, use_global_device_ids=true | all-gather | bytes 614400 | tf_op jit(solution)/shard_map/all_gather | solution.py:48
  48.6 44.5 %all-gather.12.cloned.1.call-done = bf16[32,2,2,40,2,192]{5,3,4,2,1,0:T(8,128)(2,1)} async-done(((bf16[4,2,2,40,2,192]{5,3,4,2,1,0:T(8,128)(2,1)}), bf16[32,2,2,40,2,192]{5,3,4,2,1,0:T(8,128)(2,1)}) %all-gather.12.cloned.1.call-update) | async-done | bytes 3932176 | tf_op jit(solution)/shard_map/all_gather | solution.py:48
  93.0 2.9 copy.216
  98.5 4.2 %all-to-all-start = ((f32[4,2,40,2,192]{4,1,2,3,0:T(2,128)}), f32[4,2,40,2,192]{4,1,2,3,0:T(2,128)S(1)}, u32[]{:S(2)}, u32[]{:S(2)}) async-start(f32[4,2,40,2,192]{4,1,2,3,0:T(2,128)} %broadcast_in_dim.8), calls=%async_computation | async-start | bytes 1310720 | tf_op jit(solution)/shard_map/all_to_all | solution.py:30
  103.8 10.7 %all-to-all-done = f32[4,2,40,2,192]{4,1,2,3,0:T(2,128)S(1)} async-done(((f32[4,2,40,2,192]{4,1,2,3,0:T(2,128)}), f32[4,2,40,2,192]{4,1,2,3,0:T(2,128)S(1)}, u32[]{:S(2)}, u32[]{:S(2)}) %all-to-all-start) | async-done | bytes 491552 | tf_op jit(solution)/shard_map/all_to_all | solution.py:30
  115.2 2.4 fusion.6
  117.5 2.5 add_select_fusion.1
  122.9 2.4 fusion.7
  125.2 2.5 subtract_select_fusion.1
  127.8 1.8 fusion.116
  131.6 7.0 %all-reduce.4 = (f32[]{:T(128)}, f32[]{:T(128)}) all-reduce(f32[]{:T(128)} %multiply_reduce_fusion.2, f32[]{:T(128)} %multiply_reduce_fusion.1), channel_id=1, replica_groups=mesh['freq_0'=2,'freq_1'=2,'rcv_0'=4,'rcv_1'=8,'rcv_2'=2] {'freq_0'}, use_global_device_ids=true, to_apply=%region_1.0 | all-reduce | flops 2 | bytes 16 | tf_op jit(solution)/shard_map/psum | solution.py:41
  138.7 3.1 all-reduce.3
  141.8 11.1 %all-reduce.1 = (f32[]{:T(128)}, f32[]{:T(128)}) all-reduce(f32[]{:T(128)} %get-tuple-element.43, f32[]{:T(128)} %get-tuple-element.44), channel_id=1, replica_groups=mesh['freq_0'=2,'freq_1'=2,'rcv_0'=4,'rcv_1'=8,'rcv_2'=2] {'rcv_0'}, use_global_device_ids=true, to_apply=%region_3.0 | all-reduce | flops 2 | bytes 16 | tf_op jit(solution)/shard_map/psum | solution.py:41
  152.8 17.0 %all-reduce = (f32[]{:T(128)}, f32[]{:T(128)}) all-reduce(f32[]{:T(128)} %get-tuple-element.39, f32[]{:T(128)} %get-tuple-element.40), channel_id=1, replica_groups=mesh['freq_0'=2,'freq_1'=2,'rcv_0'=4,'rcv_1'=8,'rcv_2'=2] {'rcv_1'}, use_global_device_ids=true, to_apply=%region_4.0 | all-reduce | flops 2 | bytes 16 | tf_op jit(solution)/shard_map/psum | solution.py:41
  169.9 5.5 %all-reduce.2 = (f32[]{:T(128)}, f32[]{:T(128)}) all-reduce(f32[]{:T(128)} %get-tuple-element.37, f32[]{:T(128)} %get-tuple-element.38), channel_id=1, replica_groups=mesh['freq_0'=2,'freq_1'=2,'rcv_0'=4,'rcv_1'=8,'rcv_2'=2] {'rcv_2'}, use_global_device_ids=true, to_apply=%region_5.0 | all-reduce | flops 2 | bytes 16 | tf_op jit(solution)/shard_map/psum | solution.py:41
  177.7 14.1 %all_to_all.20 = f32[4,2,40,2,192]{4,1,2,3,0:T(2,128)S(1)} all-to-all(f32[4,2,40,2,192]{4,1,2,3,0:T(2,128)S(1)} %broadcast_in_dim.9), channel_id=1, replica_groups=mesh['freq_0'=2,'freq_1'=2,'rcv_0'=4,'rcv_1'=8,'rcv_2'=2] {'freq_0','fre..., dimensions={0} | all-to-all | bytes 983040 | tf_op jit(solution)/shard_map/all_to_all | solution.py:30
  192.5 2.4 fusion.8
  194.9 2.5 add_select_fusion
  198.8 2.4 fusion.9
  201.2 2.5 subtract_select_fusion
  205.1 1.6 fusion.110
  208.1 5.1 %all_gather.58 = bf16[2,2,40,2,192]{4,2,3,1,0:T(8,128)(2,1)S(1)} all-gather(bf16[1,2,40,2,192]{4,2,3,1,0:T(8,128)(2,1)S(1)} %copy.236), channel_id=1, replica_groups=mesh['freq_0'=2,'freq_1'=2,'rcv_0'=4,'rcv_1'=8,'rcv_2'=2] {'rcv_2'}, dimensions={0}, use_global_device_ids=true | all-gather | bytes 184320 | tf_op jit(solution)/shard_map/all_gather | solution.py:48
  213.2 13.8 %all-gather.3 = bf16[8,2,40,2,192]{4,2,3,1,0:T(8,128)(2,1)} all-gather(bf16[2,2,40,2,192]{4,2,3,1,0:T(8,128)(2,1)S(1)} %all_gather.58), channel_id=5, replica_groups=mesh['freq_0'=2,'freq_1'=2,'rcv_0'=4,'rcv_1'=8,'rcv_2'=2] {'rcv_0'}, dimensions={0}, use_global_device_ids=true | all-gather | bytes 614400 | tf_op jit(solution)/shard_map/all_gather | solution.py:48
  227.1 2.9 copy.243
  232.5 3.5 all-to-all-start.2
  236.7 11.0 %all-to-all-done.2 = f32[4,2,40,2,192]{4,1,2,3,0:T(2,128)S(1)} async-done(((f32[4,2,40,2,192]{4,1,2,3,0:T(2,128)}), f32[4,2,40,2,192]{4,1,2,3,0:T(2,128)S(1)}, u32[]{:S(2)}, u32[]{:S(2)}) %all-to-all-start.2) | async-done | bytes 491552 | tf_op jit(solution)/shard_map/all_to_all | solution.py:30
  248.4 2.4 fusion.11
  250.8 3.9 %fusion.10 = f32[64,40,192]{2,0,1:T(8,128)} fusion(f32[8,40,2,192]{3,0,1,2:T(8,128)S(1)} %reshape.244, f32[8]{0:T(128)S(1)} %add_convert_fusion, f32[64]{0:T(128)S(1)} %iota_multiply_fusion), kind=kOutput, calls=%fused_computation.25 | convolution fusion | flops 47186944 | bytes 2294784 | tf_op jit(solution)/shard_map/tf,frk->trk/dot_general | solution.py:72
  254.6 3.7 subtract_multiply_fusion
  258.3 28.5 %all-gather.14.cloned.1.call-done = bf16[32,2,2,40,2,192]{5,3,4,2,1,0:T(8,128)(2,1)} async-done(((bf16[4,2,2,40,2,192]{5,3,4,2,1,0:T(8,128)(2,1)}), bf16[32,2,2,40,2,192]{5,3,4,2,1,0:T(8,128)(2,1)}) %all-gather.14.cloned.1.call-update) | async-done | bytes 3932176 | tf_op jit(solution)/shard_map/all_gather | solution.py:48
  286.9 3.0 copy.237
  291.6 1.5 multiply_reduce_fusion
  293.2 4.3 %add_multiply_fusion = f32[64,40,192]{2,0,1:T(8,128)} fusion(f32[64,40,192]{2,0,1:T(8,128)S(1)} %copy-done.2, s32[40,192]{1,0:T(8,128)S(1)} %copy-done.5, f32[8,40,2,192]{3,0,1,2:T(8,128)S(1)} %copy-done.4, f32[8]{0:T(128)S(1)} %add_convert_fusion, f32[64]{0:T(128)S(1)} %iota_multiply_fusion), kind=kOutput, calls=%fused_computation.2 | convolution fusion | flops 49644544 | bytes 4957184 | tf_op jit(solution)/shard_map/tf,frk->trk/dot_general | solution.py:72
  297.5 7.0 %psum.115 = f32[]{:T(128)} all-reduce(f32[]{:T(128)} %multiply_reduce_fusion), channel_id=1, replica_groups=mesh['freq_0'=2,'freq_1'=2,'rcv_0'=4,'rcv_1'=8,'rcv_2'=2] {'freq_0'}, use_global_device_ids=true, to_apply=%region_13.0 | all-reduce | flops 1 | bytes 8 | tf_op jit(solution)/shard_map/psum | solution.py:41
  304.5 2.0 fusion.94
  306.5 3.3 psum.116
  309.8 2.0 fusion.108
  311.8 11.2 %psum.117 = f32[]{:T(128)} all-reduce(f32[]{:T(128)} %psum.116), channel_id=1, replica_groups=mesh['freq_0'=2,'freq_1'=2,'rcv_0'=4,'rcv_1'=8,'rcv_2'=2] {'rcv_0'}, use_global_device_ids=true, to_apply=%region_15.0 | all-reduce | flops 1 | bytes 8 | tf_op jit(solution)/shard_map/psum | solution.py:41
  323.1 3.8 fusion.106
  326.9 17.0 %psum.118 = f32[]{:T(128)} all-reduce(f32[]{:T(128)} %psum.117), channel_id=1, replica_groups=mesh['freq_0'=2,'freq_1'=2,'rcv_0'=4,'rcv_1'=8,'rcv_2'=2] {'rcv_1'}, use_global_device_ids=true, to_apply=%region_16.0 | all-reduce | flops 1 | bytes 8 | tf_op jit(solution)/shard_map/psum | solution.py:41
  343.9 2.0 fusion.96
  345.9 5.5 %psum.119 = f32[]{:T(128)} all-reduce(f32[]{:T(128)} %psum.118), channel_id=1, replica_groups=mesh['freq_0'=2,'freq_1'=2,'rcv_0'=4,'rcv_1'=8,'rcv_2'=2] {'rcv_2'}, use_global_device_ids=true, to_apply=%region_17.0 | all-reduce | flops 1 | bytes 8 | tf_op jit(solution)/shard_map/psum | solution.py:41
  355.1 8.7 %all-to-all-start.3 = ((f32[64,2,2,192]{3,2,1,0:T(2,128)}), f32[64,2,2,192]{3,2,1,0:T(2,128)S(1)}, u32[]{:S(2)}, u32[]{:S(2)}) async-start(f32[64,2,2,192]{3,2,1,0:T(2,128)} %broadcast_in_dim.11), calls=%async_computation.3 | async-start | bytes 524288 | tf_op jit(solution)/shard_map/all_to_all | solution.py:30
  363.7 1.7 copy.258
  367.8 6.5 %all-to-all-done.3 = f32[64,2,2,192]{3,2,1,0:T(2,128)S(1)} async-done(((f32[64,2,2,192]{3,2,1,0:T(2,128)}), f32[64,2,2,192]{3,2,1,0:T(2,128)S(1)}, u32[]{:S(2)}, u32[]{:S(2)}) %all-to-all-start.3) | async-done | bytes 196640 | tf_op jit(solution)/shard_map/all_to_all | solution.py:30
  (84 shorter events, 27.9 us)
Async XLA Ops:
  7.2 89.1 %copy-start = (bf16[2,2,40,2560]{3,2,1,0:T(8,128)(2,1)S(1)}, bf16[2,2,40,2560]{3,2,1,0:T(8,128)(2,1)}, u32[]{:S(2)}) copy-start(bf16[2,2,40,2560]{3,2,1,0:T(8,128)(2,1)} %param.6) | copy-start | bytes 2457604
  7.2 85.9 %all-gather.12.cloned.1.call-start = ((), (), s32[]{:S(2)}) async-start(), calls=%async_computation.4 | async-start | bytes 5898240 | tf_op jit(solution)/shard_map/all_gather | solution.py:48
  28.0 199.1 %all-gather.16.cloned.1.call-start = ((), (), s32[]{:S(2)}) async-start(), calls=%async_computation.6 | async-start | bytes 5898240 | tf_op jit(solution)/shard_map/all_gather | solution.py:48
  97.3 5.7 %copy-start.9 = (f32[2,40,2,192]{3,2,1,0:T(2,128)S(1)}, f32[2,40,2,192]{3,2,1,0:T(2,128)}, u32[]{:S(2)}) copy-start(f32[2,40,2,192]{3,2,1,0:T(2,128)} %param.11) | copy-start | bytes 368644
  98.5 16.0 %all-to-all-start = ((f32[4,2,40,2,192]{4,1,2,3,0:T(2,128)}), f32[4,2,40,2,192]{4,1,2,3,0:T(2,128)S(1)}, u32[]{:S(2)}, u32[]{:S(2)}) async-start(f32[4,2,40,2,192]{4,1,2,3,0:T(2,128)} %broadcast_in_dim.8), calls=%async_computation | async-start | bytes 1310720 | tf_op jit(solution)/shard_map/all_to_all | solution.py:30
  102.8 184.1 %all-gather.14.cloned.1.call-start = ((), (), s32[]{:S(2)}) async-start(), calls=%async_computation.5 | async-start | bytes 5898240 | tf_op jit(solution)/shard_map/all_gather | solution.py:48
  103.8 13.8 %copy-start.5 = (s32[40,192]{1,0:T(8,128)S(1)}, s32[40,192]{1,0:T(8,128)}, u32[]{:S(2)}) copy-start(s32[40,192]{1,0:T(8,128)} %param.7) | copy-start | bytes 92164
  127.8 49.0 %copy-start.10 = (f32[2,40,2,192]{3,2,1,0:T(2,128)S(1)}, f32[2,40,2,192]{3,2,1,0:T(2,128)}, u32[]{:S(2)}) copy-start(f32[2,40,2,192]{3,2,1,0:T(2,128)} %param.9) | copy-start | bytes 368644
  176.8 0.7 copy-start.6
  232.5 15.2 %all-to-all-start.2 = ((f32[4,2,40,2,192]{4,1,2,3,0:T(2,128)}), f32[4,2,40,2,192]{4,1,2,3,0:T(2,128)S(1)}, u32[]{:S(2)}, u32[]{:S(2)}) async-start(f32[4,2,40,2,192]{4,1,2,3,0:T(2,128)} %broadcast_in_dim.10), calls=%async_computation.2 | async-start | bytes 1310720 | tf_op jit(solution)/shard_map/all_to_all | solution.py:30
  248.4 2.4 copy-start.3
  289.9 3.3 copy-start.2
  289.9 3.3 copy-start.4
  291.0 0.7 copy-start.7
  311.8 32.0 %copy-start.1 = (f32[64,40,192]{2,0,1:T(8,128)S(1)}, f32[64,40,192]{2,0,1:T(8,128)}, u32[]{:S(2)}) copy-start(f32[64,40,192]{2,0,1:T(8,128)} %add_multiply_fusion) | copy-start | bytes 5898244
  323.0 29.1 %copy-start.8 = (f32[2,40,1,192]{3,1,0,2:T(8,128)S(1)}, f32[2,40,1,192]{3,1,0,2:T(8,128)}, u32[]{:S(2)}) copy-start(f32[2,40,1,192]{3,1,0,2:T(8,128)} %copy-done.7) | copy-start | bytes 184324
  355.1 19.3 %all-to-all-start.3 = ((f32[64,2,2,192]{3,2,1,0:T(2,128)}), f32[64,2,2,192]{3,2,1,0:T(2,128)S(1)}, u32[]{:S(2)}, u32[]{:S(2)}) async-start(f32[64,2,2,192]{3,2,1,0:T(2,128)} %broadcast_in_dim.11), calls=%async_computation.3 | async-start | bytes 524288 | tf_op jit(solution)/shard_map/all_to_all | solution.py:30
Sparse Core Ops, SparseCore 0:
  28.1 64.8 all-gather.11
  94.8 63.2 all-gather.15
  227.2 59.6 all-gather.13

commit v2 on v1

v2 whole, which is shorter than its diff:
```python
import cmath
import functools
import math

import jax
import jax.numpy as jnp
from jax import lax
from jax.experimental import pallas as pl
from jax.experimental.pallas import tpu as pltpu
from jax.sharding import Mesh
from jax.sharding import PartitionSpec as P

N = 2560
K = 192
F = 8
TS = 64
ROWS = 40
W = 2 * K
COLS = 640
TINY = 1e-06
AXES = ("freq_0", "freq_1", "rcv_0", "rcv_1", "rcv_2")
FREQ = AXES[:2]
RCV = AXES[2:]
MESH = pl.DeviceIdType.MESH
BF = jnp.bfloat16
F32 = jnp.float32


def swap(x):
    return jnp.concatenate([x[:, K:], x[:, :K]], axis=1)


def kernel(
    refl, starts, foc, res, dirn, grad,
    o_foc, o_res, o_dir, o_green, o_corr,
    gb, rbuf, rbig, rtmp, vtmp, acc, part, rs, fx, ta, tb, img, tr, ti, arb, cb,
    g_send, g_recv, x_send, x_recv, r_send, r_recv, s_send, s_recv, f_send, f_recv,
    a_send, a_recv, c_send, c_recv,
):
    xh, c, y, z, xl = (lax.axis_index(a) for a in AXES)
    q = xh * 2 + c
    pending = []

    def dev(**other):
        me = {"xh": xh, "c": c, "y": y, "z": z, "xl": xl}
        me.update(other)
        return tuple(me[n] for n in ("xh", "c", "y", "z", "xl"))

    def copy(src, dst, ss, rr, to):
        return pltpu.make_async_remote_copy(
            src_ref=src, dst_ref=dst, send_sem=ss, recv_sem=rr, device_id=to, device_id_type=MESH
        )

    def start(*args):
        d = copy(*args)
        d.start()
        pending.append(d)

    cell = []
    for i in range(1, 8):
        dx, dc, dl = i >> 2, (i >> 1) & 1, i & 1
        cell.append(((xh + dx) % 2, (c + dc) % 2, (xl + dl) % 2))
    cell_peers = [(dev(xh=a, c=b, xl=d), a * 4 + b * 2 + d) for a, b, d in cell]
    y_peers = [(dev(y=(y + i) % 4), (y + i) % 4) for i in (2, 1, 3)]
    z_peers = [(dev(z=(z + i) % 8), (z + i) % 8) for i in range(1, 8)]
    x_peer = dev(xl=1 - xl)

    for f in range(2):
        gb[0, f, z, xl] = dirn[f].astype(BF)
        gb[1, f, z, xl] = foc[f].astype(BF)

    barrier = pltpu.get_barrier_semaphore()
    everyone = [p for p, _ in cell_peers + y_peers + z_peers]
    for p in everyone:
        pl.semaphore_signal(barrier, inc=1, device_id=p, device_id_type=MESH)
    pl.semaphore_wait(barrier, len(everyone))

    order = [(0, 0), (1, 0), (0, 1), (1, 1)]

    def valid(s, way, f):
        return s < 4 or f == way

    def unit(k, f, a, zz):
        return gb.at[k, f, zz, xl if a == 0 else 1 - xl]

    def gsem(way, s, f, a):
        return ((way * 4 + s - 1) * 2 + f) * 2 + a

    seen = set()

    def wait_unit(k, way, s, f, a):
        if (k, way, s, f, a) in seen:
            return
        seen.add((k, way, s, f, a))
        zz = (z - s + 8) % 8 if way == 0 else (z + s) % 8
        u = unit(k, f, a, zz)
        i = gsem(way, s, f, a)
        copy(u, u, g_send.at[k, i], g_recv.at[k, i], x_peer).wait_recv()

    def exchange(k):
        for f in range(2):
            u = gb.at[k, f, z, xl]
            start(u, u, x_send.at[k, f], x_recv.at[k, f], x_peer)

    def ring(k, s, sides=(0, 1)):
        for f, a in order:
            if a not in sides:
                continue
            if s == 1 and a == 1:
                u = gb.at[k, f, z, 1 - xl]
                copy(u, u, x_send.at[k, f], x_recv.at[k, f], x_peer).wait_recv()
            for way in range(2):
                if not valid(s, way, f):
                    continue
                if s > 1:
                    wait_unit(k, way, s - 1, f, a)
                zz = (z - s + 9) % 8 if way == 0 else (z + s - 1) % 8
                to = dev(z=(z + 1) % 8 if way == 0 else (z + 7) % 8)
                u = unit(k, f, a, zz)
                i = gsem(way, s, f, a)
                start(u, u, g_send.at[k, i], g_recv.at[k, i], to)

    def gathered(k):
        for s in range(1, 5):
            for f, a in order:
                for way in range(2):
                    if valid(s, way, f):
                        wait_unit(k, way, s, f, a)

    lane = lax.broadcasted_iota(jnp.int32, (8, W), 1)
    sign = jnp.where(lane < K, -1.0, 1.0).astype(F32)
    sign_rows = jnp.where(
        lax.broadcasted_iota(jnp.int32, (ROWS, W), 1) < K, -1.0, 1.0
    ).astype(F32)

    def send_reflection():
        for i, (p, yy) in enumerate(y_peers):
            cols = pl.ds(pl.multiple_of(yy * COLS, 128), COLS)
            start(refl.at[:, :, :, cols], rbuf.at[y], r_send.at[i], r_recv.at[i], p)

    def assemble_reflection():
        cols = pl.ds(pl.multiple_of(y * COLS, 128), COLS)
        for f in range(2):
            for p in range(2):
                rbuf[y, f, p] = refl[f, p, :, cols]
        for i, j in enumerate((2, 3, 1)):
            src = rbuf.at[(y + j) % 4]
            copy(src, src, r_send.at[i], r_recv.at[i], x_peer).wait_recv()
        for f in range(2):

            def put(i, _, f=f):
                rows = pl.ds(pl.multiple_of(i * ROWS, 8), ROWS)
                rtmp[rows, :] = rbuf[i // 2, f, i % 2].astype(F32)
                return 0

            lax.fori_loop(0, 8, put, 0)
            rbig[f] = rtmp[...].astype(BF)

    def multiply(k, conjugate):
        for f in range(2):

            def put(i, _, f=f):
                rows = pl.ds(pl.multiple_of(i * ROWS, 8), ROWS)
                vtmp[rows, :] = gb[k, f, i // 2, i % 2].astype(F32)
                return 0

            lax.fori_loop(0, 16, put, 0)
            acc[...] = jnp.dot(rbig[f], vtmp[...].astype(BF), preferred_element_type=F32)
            for i, (p, yy) in enumerate(y_peers + [(None, y)]):
                first = acc[pl.ds(pl.multiple_of(yy * 80, 8), ROWS), :]
                second = acc[pl.ds(pl.multiple_of(yy * 80 + 40, 8), ROWS), :]
                turned = sign_rows * swap(second)
                part[k, i, f] = first - turned if conjugate else first + turned
                if p is not None:
                    start(part.at[k, i, f], rs.at[k, y, f], s_send.at[k, i, f], s_recv.at[k, i, f], p)

    def reduced(k, f):
        total = part[k, 3, f]
        for i, j in enumerate((2, 3, 1)):
            src = rs.at[k, (y + j) % 4, f]
            copy(src, src, s_send.at[k, i, f], s_recv.at[k, i, f], x_peer).wait_recv()
            total = total + rs[k, (y + j) % 4, f]
        return total

    q_c = xh * 2 + 1 - c
    q_x = (1 - xh) * 2 + c
    q_xc = (1 - xh) * 2 + 1 - c

    def share(k):
        u = fx.at[k, q]
        start(u, u, f_send.at[k, 1], f_recv.at[k, 1], dev(xh=1 - xh))
        start(u, u, f_send.at[k, 0], f_recv.at[k, 0], dev(c=1 - c))

    def relay(k):
        u = fx.at[k, q_x]
        copy(u, u, f_send.at[k, 1], f_recv.at[k, 1], x_peer).wait_recv()
        start(u, u, f_send.at[k, 2], f_recv.at[k, 2], dev(c=1 - c))

    def shared(k):
        for i, qq in ((0, q_c), (2, q_xc)):
            u = fx.at[k, qq]
            copy(u, u, f_send.at[k, i], f_recv.at[k, i], x_peer).wait_recv()

    def band(r):
        return pl.ds(pl.multiple_of(r * 8, 8), 8)

    def tables():
        def one(r, _):
            rows = band(r)
            s = jnp.clip(starts[rows, :], 0, TS)
            zr = jnp.ones((8, W), F32)
            zi = jnp.zeros((8, W), F32)
            for b in range(6):
                w = cmath.exp(2j * math.pi * (1 << b) / TS)
                on = (s & (1 << b)) != 0
                nr, ni = zr * w.real - zi * w.imag, zr * w.imag + zi * w.real
                zr, zi = jnp.where(on, nr, zr), jnp.where(on, ni, zi)
            ta[7, rows, :] = s.astype(F32) * (1.0 / TS)
            tb[7, rows, :] = jnp.zeros((8, W), F32)
            pr, pi = zr, zi
            for d in range(1, 8):
                k = 1.0 / (TS * (1.0 - cmath.exp(2j * math.pi * d / TS)))
                gr = k.real - (k.real * pr - k.imag * pi)
                gi = sign * (k.imag - (k.real * pi + k.imag * pr))
                ta[7 + d, rows, :] = gr
                ta[7 - d, rows, :] = gr
                tb[7 + d, rows, :] = gi
                tb[7 - d, rows, :] = -gi
                pr, pi = pr * zr - pi * zi, pr * zi + pi * zr
            return 0

        lax.fori_loop(0, ROWS // 8, one, 0)

    def gate_own(fields, e, rows):
        total = None
        for j, (u, v) in enumerate(fields):
            d = 7 + j - e - 2 * q
            term = ta[d, rows, :] * u + tb[d, rows, :] * v
            total = term if total is None else total + term
        return total

    def fields_of(k, rows):
        us = [fx[k, j // 2, j % 2, rows, :] for j in range(F)]
        return [(u, swap(u)) for u in us]

    def gate_residual():
        def one(r, _):
            rows = band(r)
            fields = fields_of(0, rows)
            for e in range(2):
                tr[e, rows, :] = gate_own(fields, e, rows)
            return 0

        lax.fori_loop(0, ROWS // 8, one, 0)

    def gate_image():
        def one(r, total):
            rows = band(r)
            fields = fields_of(1, rows)
            images = []
            for j in range(F):
                t = ta[7, rows, :] * fields[j][0]
                for i in range(F):
                    if i != j:
                        d = 7 + i - j
                        t = t + ta[d, rows, :] * fields[i][0] + tb[d, rows, :] * fields[i][1]
                img[j, rows, :] = t
                images.append((t, swap(t)))
                total = total + t * t
            for e in range(2):
                ti[e, rows, :] = gate_own(images, e, rows)
            return total

        return lax.fori_loop(0, ROWS // 8, one, jnp.zeros((8, W), F32))

    def squares(load):
        def one(r, total):
            for e in range(2):
                x = load(e, band(r))
                total = total + x * x
            return total

        return lax.fori_loop(0, ROWS // 8, one, jnp.zeros((8, W), F32))

    def added(x):
        x = jnp.sum(x, axis=0, keepdims=True)
        return jnp.sum(x, axis=1, keepdims=True)

    cell_slot = xh * 4 + c * 2 + xl

    def put_sum(buf, ss, rr, slot, peers, value):
        buf[slot] = value
        for i, (p, _) in enumerate(peers):
            start(buf.at[slot], buf.at[slot], ss.at[i], rr.at[i], p)

    def get_sum(buf, ss, rr, peers, back, count):
        for i, j in enumerate(back):
            u = buf.at[j]
            copy(u, u, ss.at[i], rr.at[i], x_peer).wait_recv()
        total = buf[0]
        for i in range(1, count):
            total = total + buf[i]
        return total

    cell_back = [s for _, s in cell_peers]
    y_back = [(y + j) % 4 for j in (2, 3, 1)]
    z_back = [(z + 8 - i) % 8 for i in range(1, 8)]
    phases = [(cell_slot, cell_peers, cell_back, 8), (y, y_peers, y_back, 4), (z, z_peers, z_back, 8)]

    def sum_put(k, phase, value):
        slot, peers, _, _ = phases[phase]
        put_sum(arb.at[k, phase], a_send.at[k, phase], a_recv.at[k, phase], slot, peers, value)

    def sum_get(k, phase):
        _, peers, back, count = phases[phase]
        return get_sum(arb.at[k, phase], a_send.at[k, phase], a_recv.at[k, phase], peers, back, count)

    corr_phases = [(xl, [(x_peer, 1 - xl)], [1 - xl], 2), (y, y_peers, y_back, 4), (z, z_peers, z_back, 8)]

    def corr_put(phase, value):
        slot, peers, _, _ = corr_phases[phase]
        put_sum(cb.at[phase], c_send.at[phase], c_recv.at[phase], slot, peers, value)

    def corr_get(phase):
        _, peers, back, count = corr_phases[phase]
        return get_sum(cb.at[phase], c_send.at[phase], c_recv.at[phase], peers, back, count)

    exchange(0)
    ring(0, 1, (0,))
    send_reflection()
    fx[0, q] = res[...]
    ring(0, 1, (1,))
    exchange(1)
    share(0)
    ring(0, 2)
    tables()
    gamma_own = added(squares(lambda e, rows: grad[e, rows, :]))
    ring(0, 3)
    assemble_reflection()
    ring(0, 4)
    ring(1, 1)
    relay(0)
    gathered(0)
    multiply(0, False)
    ring(1, 2)
    for f in range(2):
        fx[1, q, f] = reduced(0, f)
    share(1)
    ring(1, 3)
    shared(0)
    gate_residual()
    relay(1)
    shared(1)
    curvature_own = added(gate_image()) * 0.25
    half = lax.broadcasted_iota(jnp.int32, (1, 128), 1) < 64
    sum_put(0, 0, jnp.where(half, gamma_own, curvature_own))
    ring(1, 4)
    sum_put(0, 1, sum_get(0, 0))
    gathered(1)
    sum_put(0, 2, sum_get(0, 1))
    both = sum_get(0, 2)
    gamma, curvature = both[:, 0:1], both[:, 64:65]
    alpha = gamma / (curvature + TINY)
    for f in range(2):
        gb[2, f, z, xl] = (tr[f] - alpha * ti[f]).astype(BF)
    exchange(2)
    ring(2, 1, (0,))
    multiply(1, False)
    ring(2, 1, (1,))
    for f in range(2):
        o_foc[f] = foc[f] + alpha * dirn[f]
        o_res[f] = res[f] - alpha * img[2 * q + f]
    ring(2, 2)
    for f in range(2):
        fx[2, q, f] = reduced(1, f)
    share(2)
    ring(2, 3)
    relay(2)
    ring(2, 4)
    shared(2)

    def green(r, total):
        rows = band(r)
        fields = fields_of(2, rows)
        out = []
        for e in range(2):
            own = fx[2, q, e, rows, :]
            g = own - gate_own(fields, e, rows)
            g = g + alpha * (fx[1, q, e, rows, :] - img[2 * q + e, rows, :])
            o_green[e, rows, :] = g
            v = o_foc[e, rows, :]
            out += [total[2 * e] + g * v, total[2 * e + 1] + g * swap(v)]
        return tuple(out)

    def finish_corr():
        none = jnp.zeros((8, W), F32)
        sums = lax.fori_loop(0, ROWS // 8, green, (none, none, none, none))
        out = []
        for e in range(2):
            a = jnp.sum(sums[2 * e], axis=0, keepdims=True)
            b = jnp.sum(sums[2 * e + 1], axis=0, keepdims=True)
            out.append(jnp.where(lane[:1] < K, a + swap(a), b - swap(b)))
        return jnp.concatenate(out, axis=0)

    gathered(2)
    multiply(2, True)
    corr_put(0, finish_corr())
    for f in range(2):
        o_dir[f] = reduced(2, f)
    sum_put(1, 0, jnp.broadcast_to(added(squares(lambda e, rows: o_dir[e, rows, :])), (1, 128)))
    corr_put(1, corr_get(0))
    sum_put(1, 1, sum_get(1, 0))
    corr_put(2, corr_get(1))
    sum_put(1, 2, sum_get(1, 1))
    o_corr[...] = corr_get(2) * (1.0 / math.sqrt(N))
    new_gamma = sum_get(1, 2)[:, 0:1]
    ratio = new_gamma / (gamma + TINY)
    for f in range(2):
        o_dir[f] = o_dir[f] + ratio * dirn[f]
    for d in pending:
        d.wait_send()


def per_device(reflection, starts, focusing, residual, direction, gradient):
    def flat(v):
        return v.reshape(2, ROWS, W)

    field = jax.ShapeDtypeStruct((2, ROWS, W), F32)
    dma = pltpu.SemaphoreType.DMA
    vmem = pl.BlockSpec(memory_space=pltpu.VMEM)
    outs = pl.pallas_call(
        kernel,
        out_shape=(field, field, field, field, jax.ShapeDtypeStruct((2, W), F32)),
        in_specs=[vmem] * 6,
        out_specs=[vmem] * 5,
        scratch_shapes=[
            pltpu.VMEM((3, 2, 8, 2, ROWS, W), BF),
            pltpu.VMEM((4, 2, 2, ROWS, COLS), BF),
            pltpu.VMEM((2, 320, COLS), BF),
            pltpu.VMEM((320, COLS), F32),
            pltpu.VMEM((COLS, W), F32),
            pltpu.VMEM((320, W), F32),
            pltpu.VMEM((3, 4, 2, ROWS, W), F32),
            pltpu.VMEM((3, 4, 2, ROWS, W), F32),
            pltpu.VMEM((3, 4, 2, ROWS, W), F32),
            pltpu.VMEM((15, ROWS, W), F32),
            pltpu.VMEM((15, ROWS, W), F32),
            pltpu.VMEM((F, ROWS, W), F32),
            pltpu.VMEM((2, ROWS, W), F32),
            pltpu.VMEM((2, ROWS, W), F32),
            pltpu.VMEM((2, 3, 8, 1, 128), F32),
            pltpu.VMEM((3, 8, 2, W), F32),
            dma((3, 32)), dma((3, 32)), dma((3, 2)), dma((3, 2)), dma((3,)), dma((3,)),
            dma((3, 3, 2)), dma((3, 3, 2)), dma((3, 3)), dma((3, 3)),
            dma((2, 3, 7)), dma((2, 3, 7)), dma((3, 7)), dma((3, 7)),
        ],
        compiler_params=pltpu.CompilerParams(
            collective_id=0, has_side_effects=True, vmem_limit_bytes=60 * 1024 * 1024
        ),
        name="marchenko",
    )(
        reflection,
        jnp.concatenate([starts, starts], axis=1),
        flat(focusing),
        flat(residual),
        flat(direction),
        flat(gradient),
    )
    shape = (2, ROWS, 2, K)
    return tuple(o.reshape(shape) for o in outs[:4]) + (outs[4].reshape(2, 2, K),)


def solution(mesh):
    finer = Mesh(mesh.devices.reshape(2, 2, 4, 8, 2), AXES)
    field = P(FREQ, RCV, None, None)
    return jax.shard_map(
        per_device,
        mesh=finer,
        in_specs=(P(FREQ, None, RCV, None), P(RCV, None), field, field, field, field),
        out_specs=(field, field, field, field, P(FREQ, None, None)),
        check_vma=False,
    )
```

time: 386 us -> 103 us (0.27)
  blocking collectives: 160 us -> 0 us
  waiting for transfers between devices: 101 us -> 0 us
  Pallas kernels: 0 us -> 90.3 us
  matrix products: 58.4 us -> 0 us
  starting transfers between devices: 16.6 us -> 0 us
  between operations: 17.1 us -> 0.66 us
  local copies, waits for them, and re-layouts: 21.5 us -> 10.1 us
  other arithmetic: 6.69 us -> 1.55 us
    pallas_call x0 -> x1, Pallas kernels: none -> 90.3 us  [per_device(): pl.pallas_call(kernel, out_shape=(field, field, field, field, jax.ShapeDt...]
    psum x10 -> x0, blocking collectives: 87.9 us -> none  [one_axis_at_a_time(): value = lax.psum(value, axis)]
    all_gather x3 -> x0, waiting for transfers between devices: 73 us -> none  [all_blocks(): pieces = lax.all_gather(pieces, axes[k])]
    dot_general x27 -> x0, matrix products: 58.4 us -> none  [the longest x12 33.8 us: contract_time(): return jnp.einsum('tf,frk->trk', table, values, precision=highest)]
    all_gather x6 -> x0, blocking collectives: 58.2 us -> none  [all_blocks(): pieces = lax.all_gather(pieces, axes[k])]
    all_to_all x3 -> x0, waiting for transfers between devices: 28.3 us -> none  [sent_to_all(): lax.all_to_all(jnp.broadcast_to(value[None], (count, *value.shape)), axis...]
    all_to_all x3 -> x0, starting transfers between devices: 16.4 us -> none  [sent_to_all(): lax.all_to_all(jnp.broadcast_to(value[None], (count, *value.shape)), axis...]
    all_to_all x1 -> x0, blocking collectives: 14.1 us -> none  [sent_to_all(): lax.all_to_all(jnp.broadcast_to(value[None], (count, *value.shape)), axis...]
  transfers between devices with their start and end apart: 6 -> 0, of which waited for: 5 -> 0; matrix products, arithmetic and copies ran while one was open for 16% -> 0% of each run, Pallas kernels for 0% -> 0%
where the time goes in v2:
time: 103 us
  Pallas kernels  90.3 us (88%)
  local copies, waits for them, and re-layouts  10.1 us (10%)
  other arithmetic  1.55 us (2%)
    pallas_call x1, Pallas kernels, per_device(): pl.pallas_call(kernel, out_shape=(field, field, field, field, jax.ShapeDt...  90.3 us
    reshape x4, local copies, waits for them, and re-layouts, per_device(): o.reshape(shape)  4.23 us
    reshape x4, local copies, waits for them, and re-layouts, flat(): return v.reshape(2, ROWS, W)  4.16 us

profile of v2, /device:TPU:32, one launch (start us, length us, event | category | flops | bytes accessed | tf_op | source)
XLA Modules:
  0.0 102.6 jit_solution(508815095623788049)
XLA Ops:
  0.6 1.6 %pad_add_fusion.starts = s32[40,384]{1,0:T(8,128)} fusion(s32[40,192]{1,0:T(8,128)} %param.7), kind=kLoop, calls=%fused_computation | loop fusion | flops 15360 | bytes 92160 | tf_op jit(solution)/shard_map/concatenate | solution.py:463
  2.2 0.0 copy-start
  2.2 1.8 %reshape.37.foc = f32[2,40,384]{2,1,0:T(8,128)} reshape(f32[2,40,2,192]{3,2,1,0:T(2,128)} %param.8) | data formatting | bytes 245760 | tf_op jit(solution)/shard_map/reshape | solution.py:426
  3.9 0.0 copy-done
  3.9 0.0 copy-start.1
  3.9 0.8 reshape.38.res
  4.7 0.1 copy-done.1
  4.9 0.0 copy-start.2
  4.9 0.8 reshape.39.dirn
  5.7 0.1 copy-done.2
  5.8 0.8 reshape.40.grad
  6.6 90.3 %marchenko.1 = (f32[2,40,384]{2,1,0:T(8,128)}, f32[2,40,384]{2,1,0:T(8,128)}, f32[2,40,384]{2,1,0:T(8,128)}, f32[2,40,384]{2,1,0:T(8,128)}, f32[2,384]{1,0:T(2,128)}) custom-call(bf16[2,2,40,2560]{3,2,1,0:T(8,128)(2,1)} %refl.1, s32[40,384]{1,0:T(8,128)} %pad_add_fusion.starts, f32[2,40,384]{2,1,0:T(8,128)} %reshape.37.foc, f32[2,40,384]{2,1,0:T(8,128)} %reshape.38.res, ...), custom_call_target="tpu_custom_call" | custom-call | tf_op jit(solution)/shard_map/marchenko/pallas_call | solution.py:431
  96.9 0.0 copy-start.6
  96.9 0.7 copy-done.6
  97.5 0.7 reshape.45
  98.2 0.0 copy-start.5
  98.2 1.8 %reshape.41 = f32[2,40,2,192]{3,2,1,0:T(2,128)} reshape(f32[2,40,384]{2,1,0:T(8,128)} %get-tuple-element.10) | data formatting | bytes 245760 | tf_op jit(solution)/shard_map/reshape | solution.py:470
  100.0 0.0 copy-done.5
  100.0 0.0 copy-start.4
  100.0 0.8 reshape.42
  100.8 0.1 copy-done.4
  100.9 0.0 copy-start.3
  100.9 0.8 reshape.43
  101.7 0.1 copy-done.3
  101.8 0.8 reshape.44
Async XLA Ops:
  2.2 1.8 %copy-start = (f32[2,40,2,192]{3,2,1,0:T(2,128)S(1)}, f32[2,40,2,192]{3,2,1,0:T(2,128)}, u32[]{:S(2)}) copy-start(f32[2,40,2,192]{3,2,1,0:T(2,128)} %param.9) | copy-start | bytes 368644
  3.9 0.9 copy-start.1
  4.9 0.9 copy-start.2
  96.9 0.7 copy-start.6
  98.2 1.8 %copy-start.5 = (f32[2,40,384]{2,1,0:T(8,128)S(1)}, f32[2,40,384]{2,1,0:T(8,128)}, u32[]{:S(2)}) copy-start(f32[2,40,384]{2,1,0:T(8,128)} %get-tuple-element.11) | copy-start | bytes 368644
  100.0 0.9 copy-start.4
  100.9 0.9 copy-start.3

commit v3 on v2

--- a/solution.py
+++ b/solution.py
@@ -31,8 +31,10 @@
 
 
 def kernel(
-    refl, starts, foc, res, dirn, grad,
-    o_foc, o_res, o_dir, o_green, o_corr,
+    refl_in, starts_in, foc_in, res_in, dirn_in, grad_in,
+    foc_out, res_out, dir_out, green_out, corr_out,
+    refl, starts, foc_l, res_l, dirn_l, grad_l, foc, dirn,
+    o_foc, o_dir, s_foc, s_res, s_dir, s_green, o_corr, i_sem, o_sem,
     gb, rbuf, rbig, rtmp, vtmp, acc, part, rs, fx, ta, tb, img, tr, ti, arb, cb,
     g_send, g_recv, x_send, x_recv, r_send, r_recv, s_send, s_recv, f_send, f_recv,
     a_send, a_recv, c_send, c_recv,
@@ -62,17 +64,58 @@
         cell.append(((xh + dx) % 2, (c + dc) % 2, (xl + dl) % 2))
     cell_peers = [(dev(xh=a, c=b, xl=d), a * 4 + b * 2 + d) for a, b, d in cell]
     y_peers = [(dev(y=(y + i) % 4), (y + i) % 4) for i in (2, 1, 3)]
-    z_peers = [(dev(z=(z + i) % 8), (z + i) % 8) for i in range(1, 8)]
+    plane = [((y + i // 8) % 4, (z + i % 8) % 8) for i in range(1, 32)]
+    plane_peers = [(dev(y=a, z=b), a * 8 + b) for a, b in plane]
     x_peer = dev(xl=1 - xl)
 
-    for f in range(2):
-        gb[0, f, z, xl] = dirn[f].astype(BF)
-        gb[1, f, z, xl] = foc[f].astype(BF)
+    loads = [
+        pltpu.make_async_copy(a, b, i_sem.at[i])
+        for i, (a, b) in enumerate(
+            [(dirn_in, dirn_l), (refl_in, refl), (foc_in, foc_l), (res_in, res_l),
+             (starts_in, starts), (grad_in, grad_l)]
+        )
+    ]
+    for d in loads:
+        d.start()
+    stores = []
+
+    def store(src, dst, i):
+        d = pltpu.make_async_copy(src, dst, o_sem.at[i])
+        d.start()
+        stores.append(d)
+
+    def band(r):
+        return pl.ds(pl.multiple_of(r * 8, 8), 8)
+
+    def flatten(src, put):
+        def one(r, _):
+            for f in range(2):
+                rows = band(r)
+                put(f, rows, jnp.concatenate([src[f, rows, 0, :], src[f, rows, 1, :]], axis=1))
+            return 0
+
+        lax.fori_loop(0, ROWS // 8, one, 0)
+
+    def split(dst, f, rows, v):
+        dst[f, rows, 0, :] = v[:, :K]
+        dst[f, rows, 1, :] = v[:, K:]
 
     barrier = pltpu.get_barrier_semaphore()
-    everyone = [p for p, _ in cell_peers + y_peers + z_peers]
+    everyone = [p for p, _ in cell_peers + plane_peers]
     for p in everyone:
         pl.semaphore_signal(barrier, inc=1, device_id=p, device_id_type=MESH)
+
+    def into(dst):
+        def put(f, rows, v):
+            dst[f, rows, :] = v
+
+        return put
+
+    loads[0].wait()
+    flatten(dirn_l, into(dirn))
+    for f in range(2):
+        gb[0, f, z, xl] = dirn[f].astype(BF)
+    loads[1].wait()
     pl.semaphore_wait(barrier, len(everyone))
 
     order = [(0, 0), (1, 0), (0, 1), (1, 1)]
@@ -186,28 +229,28 @@
     q_x = (1 - xh) * 2 + c
     q_xc = (1 - xh) * 2 + 1 - c
 
-    def share(k):
-        u = fx.at[k, q]
-        start(u, u, f_send.at[k, 1], f_recv.at[k, 1], dev(xh=1 - xh))
-        start(u, u, f_send.at[k, 0], f_recv.at[k, 0], dev(c=1 - c))
+    def share(k, f):
+        u = fx.at[k, q, f]
+        start(u, u, f_send.at[k, 1, f], f_recv.at[k, 1, f], dev(xh=1 - xh))
+        start(u, u, f_send.at[k, 0, f], f_recv.at[k, 0, f], dev(c=1 - c))
 
     def relay(k):
-        u = fx.at[k, q_x]
-        copy(u, u, f_send.at[k, 1], f_recv.at[k, 1], x_peer).wait_recv()
-        start(u, u, f_send.at[k, 2], f_recv.at[k, 2], dev(c=1 - c))
+        for f in range(2):
+            u = fx.at[k, q_x, f]
+            copy(u, u, f_send.at[k, 1, f], f_recv.at[k, 1, f], x_peer).wait_recv()
+            start(u, u, f_send.at[k, 2, f], f_recv.at[k, 2, f], dev(c=1 - c))
 
     def shared(k):
         for i, qq in ((0, q_c), (2, q_xc)):
-            u = fx.at[k, qq]
-            copy(u, u, f_send.at[k, i], f_recv.at[k, i], x_peer).wait_recv()
-
-    def band(r):
-        return pl.ds(pl.multiple_of(r * 8, 8), 8)
+            for f in range(2):
+                u = fx.at[k, qq, f]
+                copy(u, u, f_send.at[k, i, f], f_recv.at[k, i, f], x_peer).wait_recv()
 
     def tables():
         def one(r, _):
             rows = band(r)
-            s = jnp.clip(starts[rows, :], 0, TS)
+            s = starts[rows, :]
+            s = jnp.clip(jnp.concatenate([s, s], axis=1), 0, TS)
             zr = jnp.ones((8, W), F32)
             zi = jnp.zeros((8, W), F32)
             for b in range(6):
@@ -303,9 +346,8 @@
         return total
 
     cell_back = [s for _, s in cell_peers]
-    y_back = [(y + j) % 4 for j in (2, 3, 1)]
-    z_back = [(z + 8 - i) % 8 for i in range(1, 8)]
-    phases = [(cell_slot, cell_peers, cell_back, 8), (y, y_peers, y_back, 4), (z, z_peers, z_back, 8)]
+    plane_back = [((y + 4 - i // 8) % 4) * 8 + (z + 8 - i % 8) % 8 for i in range(1, 32)]
+    phases = [(cell_slot, cell_peers, cell_back, 8), (y * 8 + z, plane_peers, plane_back, 32)]
 
     def sum_put(k, phase, value):
         slot, peers, _, _ = phases[phase]
@@ -315,7 +357,7 @@
         _, peers, back, count = phases[phase]
         return get_sum(arb.at[k, phase], a_send.at[k, phase], a_recv.at[k, phase], peers, back, count)
 
-    corr_phases = [(xl, [(x_peer, 1 - xl)], [1 - xl], 2), (y, y_peers, y_back, 4), (z, z_peers, z_back, 8)]
+    corr_phases = [(xl, [(x_peer, 1 - xl)], [1 - xl], 2), phases[1]]
 
     def corr_put(phase, value):
         slot, peers, _, _ = corr_phases[phase]
@@ -328,24 +370,40 @@
     exchange(0)
     ring(0, 1, (0,))
     send_reflection()
-    fx[0, q] = res[...]
+    loads[2].wait()
+    flatten(foc_l, into(foc))
+    for f in range(2):
+        gb[1, f, z, xl] = foc[f].astype(BF)
     ring(0, 1, (1,))
     exchange(1)
-    share(0)
     ring(0, 2)
+    loads[3].wait()
+    flatten(res_l, into(fx.at[0, q]))
+    for f in range(2):
+        share(0, f)
+    loads[4].wait()
     tables()
-    gamma_own = added(squares(lambda e, rows: grad[e, rows, :]))
     ring(0, 3)
     assemble_reflection()
     ring(0, 4)
     ring(1, 1)
+    loads[5].wait()
+
+    def square(r, total):
+        for f in range(2):
+            g = grad_l[f, band(r)]
+            total = total + g * g
+        return total
+
+    gamma_all = lax.fori_loop(0, ROWS // 8, square, jnp.zeros((8, 2, K), F32))
+    gamma_own = added(jnp.sum(gamma_all, axis=0))
     relay(0)
     gathered(0)
     multiply(0, False)
     ring(1, 2)
     for f in range(2):
         fx[1, q, f] = reduced(0, f)
-    share(1)
+        share(1, f)
     ring(1, 3)
     shared(0)
     gate_residual()
@@ -357,8 +415,7 @@
     ring(1, 4)
     sum_put(0, 1, sum_get(0, 0))
     gathered(1)
-    sum_put(0, 2, sum_get(0, 1))
-    both = sum_get(0, 2)
+    both = sum_get(0, 1)
     gamma, curvature = both[:, 0:1], both[:, 64:65]
     alpha = gamma / (curvature + TINY)
     for f in range(2):
@@ -367,16 +424,28 @@
     ring(2, 1, (0,))
     multiply(1, False)
     ring(2, 1, (1,))
-    for f in range(2):
-        o_foc[f] = foc[f] + alpha * dirn[f]
-        o_res[f] = res[f] - alpha * img[2 * q + f]
+
+    def step(r, _):
+        rows = band(r)
+        for f in range(2):
+            v = foc[f, rows, :] + alpha * dirn[f, rows, :]
+            o_foc[f, rows, :] = v
+            split(s_foc, f, rows, v)
+            split(s_res, f, rows, fx[0, q, f, rows, :] - alpha * img[2 * q + f, rows, :])
+        return 0
+
+    lax.fori_loop(0, ROWS // 8, step, 0)
+    store(s_foc, foc_out, 0)
+    store(s_res, res_out, 1)
     ring(2, 2)
     for f in range(2):
         fx[2, q, f] = reduced(1, f)
-    share(2)
+        share(2, f)
     ring(2, 3)
+    ring(2, 4)
+    gathered(2)
+    multiply(2, True)
     relay(2)
-    ring(2, 4)
     shared(2)
 
     def green(r, total):
@@ -387,7 +456,7 @@
             own = fx[2, q, e, rows, :]
             g = own - gate_own(fields, e, rows)
             g = g + alpha * (fx[1, q, e, rows, :] - img[2 * q + e, rows, :])
-            o_green[e, rows, :] = g
+            split(s_green, e, rows, g)
             v = o_foc[e, rows, :]
             out += [total[2 * e] + g * v, total[2 * e + 1] + g * swap(v)]
         return tuple(out)
@@ -402,38 +471,66 @@
             out.append(jnp.where(lane[:1] < K, a + swap(a), b - swap(b)))
         return jnp.concatenate(out, axis=0)
 
-    gathered(2)
-    multiply(2, True)
     corr_put(0, finish_corr())
+    store(s_green, green_out, 2)
     for f in range(2):
         o_dir[f] = reduced(2, f)
     sum_put(1, 0, jnp.broadcast_to(added(squares(lambda e, rows: o_dir[e, rows, :])), (1, 128)))
     corr_put(1, corr_get(0))
     sum_put(1, 1, sum_get(1, 0))
-    corr_put(2, corr_get(1))
-    sum_put(1, 2, sum_get(1, 1))
-    o_corr[...] = corr_get(2) * (1.0 / math.sqrt(N))
-    new_gamma = sum_get(1, 2)[:, 0:1]
+    corr = corr_get(1) * (1.0 / math.sqrt(N))
+    for f in range(2):
+        o_corr[f, 0:1, :] = corr[f : f + 1, :K]
+        o_corr[f, 1:2, :] = corr[f : f + 1, K:]
+    store(o_corr, corr_out, 3)
+    new_gamma = sum_get(1, 1)[:, 0:1]
     ratio = new_gamma / (gamma + TINY)
-    for f in range(2):
-        o_dir[f] = o_dir[f] + ratio * dirn[f]
+
+    def last(r, _):
+        rows = band(r)
+        for f in range(2):
+            split(s_dir, f, rows, o_dir[f, rows, :] + ratio * dirn[f, rows, :])
+        return 0
+
+    lax.fori_loop(0, ROWS // 8, last, 0)
+    store(s_dir, dir_out, 4)
     for d in pending:
         d.wait_send()
+    for d in stores:
+        d.wait()
+
+
+def emit(*refs):
+    ins, outs, held, (i_sem, o_sem) = refs[:5], refs[5:10], refs[10:15], refs[15:]
+    loads = [pltpu.make_async_copy(ins[i], held[i], i_sem.at[i]) for i in range(5)]
+    stores = [pltpu.make_async_copy(held[i], outs[i], o_sem.at[i]) for i in range(5)]
+    for d in loads:
+        d.start()
+    for a, b in zip(loads, stores):
+        a.wait()
+        b.start()
+    for d in stores:
+        d.wait()
 
 
 def per_device(reflection, starts, focusing, residual, direction, gradient):
-    def flat(v):
-        return v.reshape(2, ROWS, W)
-
-    field = jax.ShapeDtypeStruct((2, ROWS, W), F32)
+    field = jax.ShapeDtypeStruct((2, ROWS, 2, K), F32)
     dma = pltpu.SemaphoreType.DMA
-    vmem = pl.BlockSpec(memory_space=pltpu.VMEM)
+    native = pltpu.VMEM((2, ROWS, 2, K), F32)
+    flat = pltpu.VMEM((2, ROWS, W), F32)
+    hbm = pl.BlockSpec(memory_space=pltpu.HBM)
+    shapes = (field, field, field, field, jax.ShapeDtypeStruct((2, 2, K), F32))
     outs = pl.pallas_call(
         kernel,
-        out_shape=(field, field, field, field, jax.ShapeDtypeStruct((2, W), F32)),
-        in_specs=[vmem] * 6,
-        out_specs=[vmem] * 5,
+        out_shape=shapes,
+        in_specs=[hbm] * 6,
+        out_specs=[hbm] * 5,
         scratch_shapes=[
+            pltpu.VMEM((2, 2, ROWS, N), BF),
+            pltpu.VMEM((ROWS, K), jnp.int32),
+            native, native, native, native, flat, flat,
+            flat, flat, native, native, native, native,
+            pltpu.VMEM((2, 2, K), F32), dma((6,)), dma((5,)),
             pltpu.VMEM((3, 2, 8, 2, ROWS, W), BF),
             pltpu.VMEM((4, 2, 2, ROWS, COLS), BF),
             pltpu.VMEM((2, 320, COLS), BF),
@@ -448,26 +545,28 @@
             pltpu.VMEM((F, ROWS, W), F32),
             pltpu.VMEM((2, ROWS, W), F32),
             pltpu.VMEM((2, ROWS, W), F32),
-            pltpu.VMEM((2, 3, 8, 1, 128), F32),
-            pltpu.VMEM((3, 8, 2, W), F32),
+            pltpu.VMEM((2, 2, 32, 1, 128), F32),
+            pltpu.VMEM((2, 32, 2, W), F32),
             dma((3, 32)), dma((3, 32)), dma((3, 2)), dma((3, 2)), dma((3,)), dma((3,)),
-            dma((3, 3, 2)), dma((3, 3, 2)), dma((3, 3)), dma((3, 3)),
-            dma((2, 3, 7)), dma((2, 3, 7)), dma((3, 7)), dma((3, 7)),
+            dma((3, 3, 2)), dma((3, 3, 2)), dma((3, 3, 2)), dma((3, 3, 2)),
+            dma((2, 2, 31)), dma((2, 2, 31)), dma((2, 31)), dma((2, 31)),
         ],
         compiler_params=pltpu.CompilerParams(
-            collective_id=0, has_side_effects=True, vmem_limit_bytes=60 * 1024 * 1024
+            collective_id=0, has_side_effects=True, vmem_limit_bytes=63 * 1024 * 1024
         ),
         name="marchenko",
-    )(
-        reflection,
-        jnp.concatenate([starts, starts], axis=1),
-        flat(focusing),
-        flat(residual),
-        flat(direction),
-        flat(gradient),
-    )
-    shape = (2, ROWS, 2, K)
-    return tuple(o.reshape(shape) for o in outs[:4]) + (outs[4].reshape(2, 2, K),)
+    )(reflection, starts, focusing, residual, direction, gradient)
+    return pl.pallas_call(
+        emit,
+        out_shape=shapes,
+        in_specs=[hbm] * 5,
+        out_specs=[hbm] * 5,
+        scratch_shapes=[
+            native, native, native, native, pltpu.VMEM((2, 2, K), F32), dma((5,)), dma((5,)),
+        ],
+        compiler_params=pltpu.CompilerParams(vmem_limit_bytes=63 * 1024 * 1024),
+        name="emit",
+    )(*outs)
 
 
 def solution(mesh):

time: 103 us -> 92.5 us (0.90)
  local copies, waits for them, and re-layouts: 10.1 us -> 0 us
  other arithmetic: 1.55 us -> 0 us
    reshape x9 -> x0, local copies, waits for them, and re-layouts: 9.06 us -> none  [the longest x4 4.23 us: per_device(): o.reshape(shape)]
    concatenate x1 -> x0, other arithmetic: 1.55 us -> none  [per_device(): jnp.concatenate([starts, starts], axis=1)]
    unnamed x14 -> x0, local copies, waits for them, and re-layouts: 1.06 us -> none
    pallas_call x1 -> x2, Pallas kernels: 90.3 us -> 91.1 us  [the longest x1 89.2 us: per_device(): pl.pallas_call(kernel, out_shape=shapes, in_specs=[hbm] * 6, out_specs=[h...]
where the time goes in v3:
time: 92.5 us; the launch traced here: 91.7 us
  Pallas kernels  91.1 us (98%)
    pallas_call x1, Pallas kernels, per_device(): pl.pallas_call(kernel, out_shape=shapes, in_specs=[hbm] * 6, out_specs=[h...  89.2 us
    pallas_call x1, Pallas kernels, per_device(): pl.pallas_call(emit, out_shape=shapes, in_specs=[hbm] * 5, out_specs=[hbm...  1.91 us

profile of v3, /device:TPU:32, one launch (start us, length us, event | category | flops | bytes accessed | tf_op | source)
XLA Modules:
  0.0 91.7 jit_solution(16922813565248356159)
XLA Ops:
  0.6 89.2 %marchenko.1 = (f32[2,40,2,192]{3,2,1,0:T(2,128)}, f32[2,40,2,192]{3,2,1,0:T(2,128)}, f32[2,40,2,192]{3,2,1,0:T(2,128)}, f32[2,40,2,192]{3,2,1,0:T(2,128)}, f32[2,2,192]{2,1,0:T(2,128)}) custom-call(bf16[2,2,40,2560]{3,2,1,0:T(8,128)(2,1)} %refl_in.1, s32[40,192]{1,0:T(8,128)} %starts_in.1, f32[2,40,2,192]{3,2,1,0:T(2,128)} %foc_in.1, ...), custom_call_target="tpu_custom_call" | custom-call | tf_op jit(solution)/shard_map/marchenko/pallas_call | solution.py:523
  89.8 1.9 %emit.1 = (f32[2,40,2,192]{3,2,1,0:T(2,128)}, f32[2,40,2,192]{3,2,1,0:T(2,128)}, f32[2,40,2,192]{3,2,1,0:T(2,128)}, f32[2,40,2,192]{3,2,1,0:T(2,128)}, f32[2,2,192]{2,1,0:T(2,128)}) custom-call(f32[2,40,2,192]{3,2,1,0:T(2,128)} %get-tuple-element.10.refs_0_, f32[2,40,2,192]{3,2,1,0:T(2,128)} %get-tuple-element.11.refs_1_, ...), custom_call_target="tpu_custom_call" | custom-call | tf_op jit(solution)/shard_map/emit/pallas_call | solution.py:559

commit v4 on v3

--- a/solution.py
+++ b/solution.py
@@ -37,11 +37,10 @@
     o_foc, o_dir, s_foc, s_res, s_dir, s_green, o_corr, i_sem, o_sem,
     gb, rbuf, rbig, rtmp, vtmp, acc, part, rs, fx, ta, tb, img, tr, ti, arb, cb,
     g_send, g_recv, x_send, x_recv, r_send, r_recv, s_send, s_recv, f_send, f_recv,
-    a_send, a_recv, c_send, c_recv,
+    a_send, a_recv, c_send, c_recv, bb, b_send, b_recv,
 ):
     xh, c, y, z, xl = (lax.axis_index(a) for a in AXES)
     q = xh * 2 + c
-    pending = []
 
     def dev(**other):
         me = {"xh": xh, "c": c, "y": y, "z": z, "xl": xl}
@@ -54,9 +53,13 @@
         )
 
     def start(*args):
-        d = copy(*args)
-        d.start()
-        pending.append(d)
+        copy(*args).start()
+
+    def sent(ref, sem):
+        copy(ref, ref, sem, sem, x_peer).wait_send()
+
+    def came(ref, sem):
+        copy(ref, ref, sem, sem, x_peer).wait_recv()
 
     cell = []
     for i in range(1, 8):
@@ -67,6 +70,8 @@
     plane = [((y + i // 8) % 4, (z + i % 8) % 8) for i in range(1, 32)]
     plane_peers = [(dev(y=a, z=b), a * 8 + b) for a, b in plane]
     x_peer = dev(xl=1 - xl)
+    block = [((xl + i // 32) % 2, (y + i // 8 % 4) % 4, (z + i % 8) % 8) for i in range(1, 64)]
+    block_peers = [(dev(xl=a, y=b, z=d), (b * 8 + d) * 2 + a) for a, b, d in block]
 
     loads = [
         pltpu.make_async_copy(a, b, i_sem.at[i])
@@ -101,7 +106,8 @@
         dst[f, rows, 1, :] = v[:, K:]
 
     barrier = pltpu.get_barrier_semaphore()
-    everyone = [p for p, _ in cell_peers + plane_peers]
+    near = [dev(z=(z + i) % 8, xl=a) for i in (1, 7) for a in (xl, 1 - xl)]
+    everyone = [p for p, _ in cell_peers + y_peers] + near
     for p in everyone:
         pl.semaphore_signal(barrier, inc=1, device_id=p, device_id_type=MESH)
 
@@ -127,7 +133,7 @@
         return gb.at[k, f, zz, xl if a == 0 else 1 - xl]
 
     def gsem(way, s, f, a):
-        return ((way * 4 + s - 1) * 2 + f) * 2 + a
+        return (way * 3 + s - 1) * 4 + f * 2 + a if s < 4 else 24 + way * 2 + a
 
     seen = set()
 
@@ -138,33 +144,54 @@
         zz = (z - s + 8) % 8 if way == 0 else (z + s) % 8
         u = unit(k, f, a, zz)
         i = gsem(way, s, f, a)
-        copy(u, u, g_send.at[k, i], g_recv.at[k, i], x_peer).wait_recv()
+        fresh.append((k, f, zz, xl if a == 0 else 1 - xl))
+        came(u, g_recv.at[k, i])
 
     def exchange(k):
         for f in range(2):
             u = gb.at[k, f, z, xl]
-            start(u, u, x_send.at[k, f], x_recv.at[k, f], x_peer)
+            start(u, u, x_send.at[k], x_recv.at[k], x_peer)
 
     def ring(k, s, sides=(0, 1)):
         for f, a in order:
             if a not in sides:
                 continue
-            if s == 1 and a == 1:
-                u = gb.at[k, f, z, 1 - xl]
-                copy(u, u, x_send.at[k, f], x_recv.at[k, f], x_peer).wait_recv()
             for way in range(2):
                 if not valid(s, way, f):
                     continue
                 if s > 1:
                     wait_unit(k, way, s - 1, f, a)
                 zz = (z - s + 9) % 8 if way == 0 else (z + s - 1) % 8
-                to = dev(z=(z + 1) % 8 if way == 0 else (z + 7) % 8)
-                u = unit(k, f, a, zz)
+                far = (z + 1) % 8 if way == 0 else (z + 7) % 8
                 i = gsem(way, s, f, a)
-                start(u, u, g_send.at[k, i], g_recv.at[k, i], to)
+                if s == 1:
+                    u = gb.at[k, f, z, xl]
+                    to = dev(z=far) if a == 0 else dev(z=far, xl=1 - xl)
+                else:
+                    u = unit(k, f, a, zz)
+                    to = dev(z=far)
+                start(u, u, g_send.at[k], g_recv.at[k, i], to)
+
+    def lay(k, f, zz, xx):
+        i = zz * 2 + xx
+        rows = pl.ds(pl.multiple_of(i * ROWS, 8), ROWS)
+        vtmp[f, rows, :] = gb[k, f, zz, xx].astype(F32)
+
+    fresh = []
+
+    def drain(k):
+        for kk, f, zz, xx in [v for v in fresh if v[0] == k]:
+            lay(k, f, zz, xx)
+        fresh[:] = [v for v in fresh if v[0] != k]
 
     def gathered(k):
+        came(gb.at[k, :, z, 1 - xl], x_recv.at[k])
+        for f in range(2):
+            fresh.append((k, f, z, 1 - xl))
+            fresh.append((k, f, z, xl))
         for s in range(1, 5):
+            if s == 4:
+                drain(k) if k != 1 else None
             for f, a in order:
                 for way in range(2):
                     if valid(s, way, f):
@@ -177,18 +204,16 @@
     ).astype(F32)
 
     def send_reflection():
-        for i, (p, yy) in enumerate(y_peers):
+        for p, yy in y_peers:
             cols = pl.ds(pl.multiple_of(yy * COLS, 128), COLS)
-            start(refl.at[:, :, :, cols], rbuf.at[y], r_send.at[i], r_recv.at[i], p)
+            start(refl.at[:, :, :, cols], rbuf.at[y], r_send, r_recv, p)
 
     def assemble_reflection():
         cols = pl.ds(pl.multiple_of(y * COLS, 128), COLS)
         for f in range(2):
             for p in range(2):
                 rbuf[y, f, p] = refl[f, p, :, cols]
-        for i, j in enumerate((2, 3, 1)):
-            src = rbuf.at[(y + j) % 4]
-            copy(src, src, r_send.at[i], r_recv.at[i], x_peer).wait_recv()
+        came(rbuf.at[0:3], r_recv)
         for f in range(2):
 
             def put(i, _, f=f):
@@ -200,28 +225,21 @@
             rbig[f] = rtmp[...].astype(BF)
 
     def multiply(k, conjugate):
-        for f in range(2):
-
-            def put(i, _, f=f):
-                rows = pl.ds(pl.multiple_of(i * ROWS, 8), ROWS)
-                vtmp[rows, :] = gb[k, f, i // 2, i % 2].astype(F32)
-                return 0
-
-            lax.fori_loop(0, 16, put, 0)
-            acc[...] = jnp.dot(rbig[f], vtmp[...].astype(BF), preferred_element_type=F32)
+        drain(k)
+        for f in range(2):
+            acc[...] = jnp.dot(rbig[f], vtmp[f].astype(BF), preferred_element_type=F32)
             for i, (p, yy) in enumerate(y_peers + [(None, y)]):
                 first = acc[pl.ds(pl.multiple_of(yy * 80, 8), ROWS), :]
                 second = acc[pl.ds(pl.multiple_of(yy * 80 + 40, 8), ROWS), :]
                 turned = sign_rows * swap(second)
                 part[k, i, f] = first - turned if conjugate else first + turned
                 if p is not None:
-                    start(part.at[k, i, f], rs.at[k, y, f], s_send.at[k, i, f], s_recv.at[k, i, f], p)
+                    start(part.at[k, i, f], rs.at[k, y, f], s_send.at[k], s_recv.at[k, f], p)
 
     def reduced(k, f):
         total = part[k, 3, f]
-        for i, j in enumerate((2, 3, 1)):
-            src = rs.at[k, (y + j) % 4, f]
-            copy(src, src, s_send.at[k, i, f], s_recv.at[k, i, f], x_peer).wait_recv()
+        came(rs.at[k, 0:3, f], s_recv.at[k, f])
+        for j in (2, 3, 1):
             total = total + rs[k, (y + j) % 4, f]
         return total
 
@@ -231,20 +249,17 @@
 
     def share(k, f):
         u = fx.at[k, q, f]
-        start(u, u, f_send.at[k, 1, f], f_recv.at[k, 1, f], dev(xh=1 - xh))
-        start(u, u, f_send.at[k, 0, f], f_recv.at[k, 0, f], dev(c=1 - c))
+        start(u, u, f_send.at[k], f_recv.at[k, f], dev(xh=1 - xh))
+        start(u, u, f_send.at[k], f_recv.at[k, 2], dev(c=1 - c))
 
     def relay(k):
         for f in range(2):
             u = fx.at[k, q_x, f]
-            copy(u, u, f_send.at[k, 1, f], f_recv.at[k, 1, f], x_peer).wait_recv()
-            start(u, u, f_send.at[k, 2, f], f_recv.at[k, 2, f], dev(c=1 - c))
+            came(u, f_recv.at[k, f])
+            start(u, u, f_send.at[k], f_recv.at[k, 2], dev(c=1 - c))
 
     def shared(k):
-        for i, qq in ((0, q_c), (2, q_xc)):
-            for f in range(2):
-                u = fx.at[k, qq, f]
-                copy(u, u, f_send.at[k, i, f], f_recv.at[k, i, f], x_peer).wait_recv()
+        came(fx.at[k, 0:2], f_recv.at[k, 2])
 
     def tables():
         def one(r, _):
@@ -333,60 +348,56 @@
 
     def put_sum(buf, ss, rr, slot, peers, value):
         buf[slot] = value
-        for i, (p, _) in enumerate(peers):
-            start(buf.at[slot], buf.at[slot], ss.at[i], rr.at[i], p)
-
-    def get_sum(buf, ss, rr, peers, back, count):
-        for i, j in enumerate(back):
-            u = buf.at[j]
-            copy(u, u, ss.at[i], rr.at[i], x_peer).wait_recv()
+        for p, _ in peers:
+            start(buf.at[slot], buf.at[slot], ss, rr, p)
+
+    def get_sum(buf, ss, rr, count):
+        came(buf.at[0 : count - 1], rr)
+        sent(buf.at[0 : count - 1], ss)
         total = buf[0]
         for i in range(1, count):
             total = total + buf[i]
         return total
 
-    cell_back = [s for _, s in cell_peers]
-    plane_back = [((y + 4 - i // 8) % 4) * 8 + (z + 8 - i % 8) % 8 for i in range(1, 32)]
-    phases = [(cell_slot, cell_peers, cell_back, 8), (y * 8 + z, plane_peers, plane_back, 32)]
+    phases = [(cell_slot, cell_peers, 8), (y * 8 + z, plane_peers, 32)]
 
     def sum_put(k, phase, value):
-        slot, peers, _, _ = phases[phase]
+        slot, peers, _ = phases[phase]
         put_sum(arb.at[k, phase], a_send.at[k, phase], a_recv.at[k, phase], slot, peers, value)
 
     def sum_get(k, phase):
-        _, peers, back, count = phases[phase]
-        return get_sum(arb.at[k, phase], a_send.at[k, phase], a_recv.at[k, phase], peers, back, count)
-
-    corr_phases = [(xl, [(x_peer, 1 - xl)], [1 - xl], 2), phases[1]]
+        return get_sum(arb.at[k, phase], a_send.at[k, phase], a_recv.at[k, phase], phases[phase][2])
+
+    corr_phases = [(xl, [(x_peer, 1 - xl)], 2), phases[1]]
 
     def corr_put(phase, value):
-        slot, peers, _, _ = corr_phases[phase]
+        slot, peers, _ = corr_phases[phase]
         put_sum(cb.at[phase], c_send.at[phase], c_recv.at[phase], slot, peers, value)
 
     def corr_get(phase):
-        _, peers, back, count = corr_phases[phase]
-        return get_sum(cb.at[phase], c_send.at[phase], c_recv.at[phase], peers, back, count)
-
+        return get_sum(cb.at[phase], c_send.at[phase], c_recv.at[phase], corr_phases[phase][2])
+
+    ring(0, 1)
     exchange(0)
-    ring(0, 1, (0,))
     send_reflection()
     loads[2].wait()
     flatten(foc_l, into(foc))
     for f in range(2):
         gb[1, f, z, xl] = foc[f].astype(BF)
-    ring(0, 1, (1,))
-    exchange(1)
     ring(0, 2)
     loads[3].wait()
     flatten(res_l, into(fx.at[0, q]))
     for f in range(2):
         share(0, f)
     loads[4].wait()
+    ring(0, 3)
+    drain(0)
     tables()
-    ring(0, 3)
-    assemble_reflection()
     ring(0, 4)
     ring(1, 1)
+    exchange(1)
+    drain(0)
+    assemble_reflection()
     loads[5].wait()
 
     def square(r, total):
@@ -397,6 +408,7 @@
 
     gamma_all = lax.fori_loop(0, ROWS // 8, square, jnp.zeros((8, 2, K), F32))
     gamma_own = added(jnp.sum(gamma_all, axis=0))
+    sum_put(0, 0, jnp.broadcast_to(gamma_own, (1, 128)))
     relay(0)
     gathered(0)
     multiply(0, False)
@@ -404,26 +416,25 @@
     for f in range(2):
         fx[1, q, f] = reduced(0, f)
         share(1, f)
+    sum_put(0, 1, sum_get(0, 0))
     ring(1, 3)
     shared(0)
     gate_residual()
     relay(1)
     shared(1)
-    curvature_own = added(gate_image()) * 0.25
-    half = lax.broadcasted_iota(jnp.int32, (1, 128), 1) < 64
-    sum_put(0, 0, jnp.where(half, gamma_own, curvature_own))
+    curvature_own = added(gate_image())
+    block_slot = (y * 8 + z) * 2 + xl
+    put_sum(bb, b_send, b_recv, block_slot, block_peers, jnp.broadcast_to(curvature_own, (1, 128)))
     ring(1, 4)
-    sum_put(0, 1, sum_get(0, 0))
+    gamma = sum_get(0, 1)[:, 0:1]
     gathered(1)
-    both = sum_get(0, 1)
-    gamma, curvature = both[:, 0:1], both[:, 64:65]
+    curvature = get_sum(bb, b_send, b_recv, 64)[:, 0:1]
     alpha = gamma / (curvature + TINY)
     for f in range(2):
         gb[2, f, z, xl] = (tr[f] - alpha * ti[f]).astype(BF)
+    ring(2, 1)
     exchange(2)
-    ring(2, 1, (0,))
     multiply(1, False)
-    ring(2, 1, (1,))
 
     def step(r, _):
         rows = band(r)
@@ -434,15 +445,18 @@
             split(s_res, f, rows, fx[0, q, f, rows, :] - alpha * img[2 * q + f, rows, :])
         return 0
 
+    ring(2, 2)
     lax.fori_loop(0, ROWS // 8, step, 0)
     store(s_foc, foc_out, 0)
     store(s_res, res_out, 1)
-    ring(2, 2)
+    drain(2)
     for f in range(2):
         fx[2, q, f] = reduced(1, f)
         share(2, f)
     ring(2, 3)
+    drain(2)
     ring(2, 4)
+    drain(2)
     gathered(2)
     multiply(2, True)
     relay(2)
@@ -494,8 +508,12 @@
 
     lax.fori_loop(0, ROWS // 8, last, 0)
     store(s_dir, dir_out, 4)
-    for d in pending:
-        d.wait_send()
+    sent(rbuf.at[0:3], r_send)
+    for k in range(3):
+        sent(gb.at[k, :, 0:7], g_send.at[k])
+        sent(gb.at[k, :, 0, 0], x_send.at[k])
+        sent(part.at[k, 0:3], s_send.at[k])
+        sent(fx.at[k, 0:3], f_send.at[k])
     for d in stores:
         d.wait()
 
@@ -535,7 +553,7 @@
             pltpu.VMEM((4, 2, 2, ROWS, COLS), BF),
             pltpu.VMEM((2, 320, COLS), BF),
             pltpu.VMEM((320, COLS), F32),
-            pltpu.VMEM((COLS, W), F32),
+            pltpu.VMEM((2, COLS, W), F32),
             pltpu.VMEM((320, W), F32),
             pltpu.VMEM((3, 4, 2, ROWS, W), F32),
             pltpu.VMEM((3, 4, 2, ROWS, W), F32),
@@ -547,9 +565,10 @@
             pltpu.VMEM((2, ROWS, W), F32),
             pltpu.VMEM((2, 2, 32, 1, 128), F32),
             pltpu.VMEM((2, 32, 2, W), F32),
-            dma((3, 32)), dma((3, 32)), dma((3, 2)), dma((3, 2)), dma((3,)), dma((3,)),
-            dma((3, 3, 2)), dma((3, 3, 2)), dma((3, 3, 2)), dma((3, 3, 2)),
-            dma((2, 2, 31)), dma((2, 2, 31)), dma((2, 31)), dma((2, 31)),
+            dma((3,)), dma((3, 28)), dma((3,)), dma((3,)), dma, dma,
+            dma((3,)), dma((3, 2)), dma((3,)), dma((3, 3)),
+            dma((2, 2)), dma((2, 2)), dma((2,)), dma((2,)),
+            pltpu.VMEM((64, 1, 128), F32), dma, dma,
         ],
         compiler_params=pltpu.CompilerParams(
             collective_id=0, has_side_effects=True, vmem_limit_bytes=63 * 1024 * 1024

time: 92.5 us -> 81.6 us (0.88)
  Pallas kernels: 91.1 us -> 79.5 us
    pallas_call x1, Pallas kernels: 89.2 us -> 77.6 us  [per_device(): pl.pallas_call(kernel, out_shape=shapes, in_specs=[hbm] * 6, out_specs=[h...]
where the time goes in v4:
time: 81.6 us; the launch traced here: 80.1 us
  Pallas kernels  79.5 us (97%)
    pallas_call x1, Pallas kernels, per_device(): pl.pallas_call(kernel, out_shape=shapes, in_specs=[hbm] * 6, out_specs=[h...  77.6 us
    pallas_call x1, Pallas kernels, per_device(): pl.pallas_call(emit, out_shape=shapes, in_specs=[hbm] * 5, out_specs=[hbm...  1.91 us

profile of v4, /device:TPU:32, one launch (start us, length us, event | category | flops | bytes accessed | tf_op | source)
XLA Modules:
  0.0 80.1 jit_solution(9619725647447394112)
XLA Ops:
  0.6 77.6 %marchenko.1 = (f32[2,40,2,192]{3,2,1,0:T(2,128)}, f32[2,40,2,192]{3,2,1,0:T(2,128)}, f32[2,40,2,192]{3,2,1,0:T(2,128)}, f32[2,40,2,192]{3,2,1,0:T(2,128)}, f32[2,2,192]{2,1,0:T(2,128)}) custom-call(bf16[2,2,40,2560]{3,2,1,0:T(8,128)(2,1)} %refl_in.1, s32[40,192]{1,0:T(8,128)} %starts_in.1, f32[2,40,2,192]{3,2,1,0:T(2,128)} %foc_in.1, ...), custom_call_target="tpu_custom_call" | custom-call | tf_op jit(solution)/shard_map/marchenko/pallas_call | solution.py:541
  78.2 1.9 %emit.1 = (f32[2,40,2,192]{3,2,1,0:T(2,128)}, f32[2,40,2,192]{3,2,1,0:T(2,128)}, f32[2,40,2,192]{3,2,1,0:T(2,128)}, f32[2,40,2,192]{3,2,1,0:T(2,128)}, f32[2,2,192]{2,1,0:T(2,128)}) custom-call(f32[2,40,2,192]{3,2,1,0:T(2,128)} %get-tuple-element.10.refs_0_, f32[2,40,2,192]{3,2,1,0:T(2,128)} %get-tuple-element.11.refs_1_, ...), custom_call_target="tpu_custom_call" | custom-call | tf_op jit(solution)/shard_map/emit/pallas_call | solution.py:578

commit v5 on v4

--- a/solution.py
+++ b/solution.py
@@ -73,6 +73,12 @@
     block = [((xl + i // 32) % 2, (y + i // 8 % 4) % 4, (z + i % 8) % 8) for i in range(1, 64)]
     block_peers = [(dev(xl=a, y=b, z=d), (b * 8 + d) * 2 + a) for a, b, d in block]
 
+    barrier = pltpu.get_barrier_semaphore()
+    near = [dev(z=(z + i) % 8, xl=a) for i in (1, 7) for a in (xl, 1 - xl)]
+    everyone = [p for p, _ in cell_peers + y_peers] + near
+    for p in everyone:
+        pl.semaphore_signal(barrier, inc=1, device_id=p, device_id_type=MESH)
+
     loads = [
         pltpu.make_async_copy(a, b, i_sem.at[i])
         for i, (a, b) in enumerate(
@@ -104,12 +110,6 @@
     def split(dst, f, rows, v):
         dst[f, rows, 0, :] = v[:, :K]
         dst[f, rows, 1, :] = v[:, K:]
-
-    barrier = pltpu.get_barrier_semaphore()
-    near = [dev(z=(z + i) % 8, xl=a) for i in (1, 7) for a in (xl, 1 - xl)]
-    everyone = [p for p, _ in cell_peers + y_peers] + near
-    for p in everyone:
-        pl.semaphore_signal(barrier, inc=1, device_id=p, device_id_type=MESH)
 
     def into(dst):
         def put(f, rows, v):
@@ -315,7 +315,6 @@
         def one(r, total):
             rows = band(r)
             fields = fields_of(1, rows)
-            images = []
             for j in range(F):
                 t = ta[7, rows, :] * fields[j][0]
                 for i in range(F):
@@ -323,13 +322,21 @@
                         d = 7 + i - j
                         t = t + ta[d, rows, :] * fields[i][0] + tb[d, rows, :] * fields[i][1]
                 img[j, rows, :] = t
-                images.append((t, swap(t)))
                 total = total + t * t
+            return total
+
+        return lax.fori_loop(0, ROWS // 8, one, jnp.zeros((8, W), F32))
+
+    def gate_again():
+        def one(r, _):
+            rows = band(r)
+            images = [img[j, rows, :] for j in range(F)]
+            images = [(u, swap(u)) for u in images]
             for e in range(2):
                 ti[e, rows, :] = gate_own(images, e, rows)
-            return total
-
-        return lax.fori_loop(0, ROWS // 8, one, jnp.zeros((8, W), F32))
+            return 0
+
+        lax.fori_loop(0, ROWS // 8, one, 0)
 
     def squares(load):
         def one(r, total):
@@ -425,6 +432,7 @@
     curvature_own = added(gate_image())
     block_slot = (y * 8 + z) * 2 + xl
     put_sum(bb, b_send, b_recv, block_slot, block_peers, jnp.broadcast_to(curvature_own, (1, 128)))
+    gate_again()
     ring(1, 4)
     gamma = sum_get(0, 1)[:, 0:1]
     gathered(1)
@@ -450,10 +458,10 @@
     store(s_foc, foc_out, 0)
     store(s_res, res_out, 1)
     drain(2)
+    ring(2, 3)
     for f in range(2):
         fx[2, q, f] = reduced(1, f)
         share(2, f)
-    ring(2, 3)
     drain(2)
     ring(2, 4)
     drain(2)

time: 81.6 us -> 79.4 us (0.973)
  Pallas kernels: 79.5 us -> 78 us
    pallas_call x1, Pallas kernels: 77.6 us -> 76.1 us  [per_device(): pl.pallas_call(kernel, out_shape=shapes, in_specs=[hbm] * 6, out_specs=[h...]
where the time goes in v5:
time: 79.4 us; the launch traced here: 78.6 us
  Pallas kernels  78 us (98%)
    pallas_call x1, Pallas kernels, per_device(): pl.pallas_call(kernel, out_shape=shapes, in_specs=[hbm] * 6, out_specs=[h...  76.1 us
    pallas_call x1, Pallas kernels, per_device(): pl.pallas_call(emit, out_shape=shapes, in_specs=[hbm] * 5, out_specs=[hbm...  1.91 us

profile of v5, /device:TPU:32, one launch (start us, length us, event | category | flops | bytes accessed | tf_op | source)
XLA Modules:
  0.0 78.6 jit_solution(16054428432876744460)
XLA Ops:
  0.6 76.1 %marchenko.1 = (f32[2,40,2,192]{3,2,1,0:T(2,128)}, f32[2,40,2,192]{3,2,1,0:T(2,128)}, f32[2,40,2,192]{3,2,1,0:T(2,128)}, f32[2,40,2,192]{3,2,1,0:T(2,128)}, f32[2,2,192]{2,1,0:T(2,128)}) custom-call(bf16[2,2,40,2560]{3,2,1,0:T(8,128)(2,1)} %refl_in.1, s32[40,192]{1,0:T(8,128)} %starts_in.1, f32[2,40,2,192]{3,2,1,0:T(2,128)} %foc_in.1, ...), custom_call_target="tpu_custom_call" | custom-call | tf_op jit(solution)/shard_map/marchenko/pallas_call | solution.py:549
  76.7 1.9 %emit.1 = (f32[2,40,2,192]{3,2,1,0:T(2,128)}, f32[2,40,2,192]{3,2,1,0:T(2,128)}, f32[2,40,2,192]{3,2,1,0:T(2,128)}, f32[2,40,2,192]{3,2,1,0:T(2,128)}, f32[2,2,192]{2,1,0:T(2,128)}) custom-call(f32[2,40,2,192]{3,2,1,0:T(2,128)} %get-tuple-element.10.refs_0_, f32[2,40,2,192]{3,2,1,0:T(2,128)} %get-tuple-element.11.refs_1_, ...), custom_call_target="tpu_custom_call" | custom-call | tf_op jit(solution)/shard_map/emit/pallas_call | solution.py:586
